TPU v7x, 256 devices: a whole 4x4x8 slice. The times are simulated.
256 devices in a mesh: vox: 64 (over x, z_lo, y, core), load: 4 (over z_hi).
Axes of the slice: x: 4, y: 4, z: 8 (z_hi: 4, z_lo: 2; z = z_hi * 2 + z_lo), core: 2. Of those that a mesh axis runs over, the one named last changes fastest.
Arguments:
- reduced_shape_matrix: bfloat16 [65536, 512], P('vox'), may hold values from -0.25 to 0.25
- young_modulus: float32 [65536], P('vox'), may hold values from 0.5 to 2
- work_stiffening_modulus: float32 [65536], P('vox'), may hold values from 0.2 to 2
- entry_flow_stress: float32 [65536], P('vox'), may hold values from 0.5 to 2
- dilation_factor: float32 [65536], P('vox'), may hold values from 0.5 to 2
- heat_difference: float32 [512], P('load'), may hold values from -4 to 4
- flowing_entry_flags: int32 [65536, 512], P('vox', 'load'), may hold values 0 or 1
- starting_permanent_deformation: float32 [65536, 512], P('vox', 'load'), may hold values from -3 to 3
- starting_weights: float32 [512, 512], P('vox', 'load'), may hold values from -5 to 5
- applied_reduced_vector: float32 [512, 512], P('vox', 'load'), may hold values from -768 to 768
- approx_tangent_inverse: float32 [512, 512], replicated, as said below
Outputs:
- final_mode_coefficients: float32 [512, 512], P('vox', 'load')
- strain_out: float32 [65536, 512], P('vox', 'load')
Inputs may be any that keep to these rules, and one draw needn't show every extreme that they name: `approx_tangent_inverse`: it has a positive diagonal.
All inputs are finite; a program needn't handle non-finite values. No bound on the sum of `flowing_entry_flags` on one device may be relied on, other than what follows from the above.
Results may differ from a plain program's by a relative error of at most 0.0013.
Values may be sent and summed in bfloat16 or wider, within the bound.
No kernel may reach another device: no remote copies, remote signals or barrier semaphores. Data moves between devices by JAX's collectives and lax.ppermute only.
A program may use at most 64 MiB of HBM per device.

v0:
```python
import jax
import jax.numpy as jnp
from jax import lax
from jax.sharding import Mesh
from jax.sharding import PartitionSpec as P

M = 512
ITERS = 3
VOX = ("vox_0", "vox_1", "vox_2", "vox_3")
VOX_LOAD = ("vox_0", "vox_1", "vox_2", "vox_3", "load")


def joined_along(pieces, dim):
    pieces = jnp.moveaxis(pieces, 0, dim)
    shape = pieces.shape
    return pieces.reshape(*shape[:dim], shape[dim] * shape[dim + 1], *shape[dim + 2 :])


def from_everyone(shard, axis):
    size = lax.axis_size(axis)
    return lax.all_to_all(
        jnp.broadcast_to(shard[None], (size, *shard.shape)), axis, 0, 0, tiled=True
    )


def collect(shard, axis, dim):
    return joined_along(from_everyone(shard, axis), dim)


def in_blocks(shard, dim, size):
    before, after = (shard.shape[:dim], shard.shape[dim + 1 :])
    return jnp.moveaxis(shard.reshape(*before, size, -1, *after), dim, 0)


def sum_at_owner(shard, axis, dim):
    size = lax.axis_size(axis)
    pieces = lax.all_to_all(in_blocks(shard, dim, size), axis, 0, 0, tiled=True)
    return jnp.sum(pieces, axis=0)


def over_axes(shard, axes):
    for axis in axes:
        shard = lax.psum(shard, axis)
    return shard


def shards(
    reduced_shape_matrix,
    young_modulus,
    work_stiffening_modulus,
    entry_flow_stress,
    dilation_factor,
    heat_difference,
    flowing_entry_flags,
    starting_permanent_deformation,
    starting_weights,
    applied_reduced_vector,
    approx_tangent_inverse,
):
    own_rows = starting_weights.shape[0]
    points = starting_weights.shape[1]
    load_point_total = points * lax.axis_size("load")
    plastic = starting_permanent_deformation
    active = flowing_entry_flags.astype(jnp.float32)
    modulus = young_modulus[:, None]
    harden = work_stiffening_modulus[:, None]
    yielded = entry_flow_stress[:, None]
    heating_history = dilation_factor[:, None] * heat_difference[None, :]
    xi_now = starting_weights
    my_precond = lax.dynamic_slice_in_dim(
        approx_tangent_inverse, lax.axis_index(VOX) * own_rows, own_rows, 0
    )
    for sweep in range(ITERS):
        xi_whole = collect(xi_now.astype(jnp.bfloat16), VOX, 0)
        strain = jnp.dot(reduced_shape_matrix, xi_whole, preferred_element_type=jnp.float32)
        trial = modulus * (strain - heating_history - plastic)
        excess = trial - yielded * jnp.tanh(trial / yielded)
        increment = active * excess / (modulus + harden)
        stress = (trial - modulus * increment).astype(jnp.bfloat16)
        stress, plastic = (stress, plastic + increment)
        partial_sum = lax.dot_general(
            reduced_shape_matrix,
            stress,
            (((0,), (0,)), ((), ())),
            preferred_element_type=jnp.float32,
        )
        resid = sum_at_owner(partial_sum, VOX, 0) - applied_reduced_vector
        resid_all = collect(resid, VOX, 0)
        delta = jnp.dot(my_precond, resid_all, precision=lax.Precision.HIGHEST)
        spread = over_axes(jnp.sum(delta * delta), VOX_LOAD) / (M * load_point_total)
        xi_now = xi_now - delta / (1.0 + spread)
    return (xi_now, plastic)


def solution(mesh):
    split = Mesh(
        mesh.devices.reshape(4, 2, 4, 2, mesh.shape["load"]),
        ("vox_0", "vox_1", "vox_2", "vox_3", "load"),
    )
    return jax.shard_map(
        shards,
        mesh=split,
        in_specs=(
            P(VOX, None),
            P(VOX),
            P(VOX),
            P(VOX),
            P(VOX),
            P("load"),
            P(VOX, "load"),
            P(VOX, "load"),
            P(VOX, "load"),
            P(VOX, "load"),
            P(),
        ),
        out_specs=(P(VOX, "load"), P(VOX, "load")),
        check_vma=False,
    )
```

profile of v0, /device:TPU:1, one launch (start us, length us, event | category | flops | bytes accessed | tf_op | source)
XLA Modules:
  0.0 263.7 jit_solution(17287310911029910719)
XLA Ops:
  2.1 10.5 %all-to-all-start = ((bf16[64,8,128]{2,1,0:T(8,128)(2,1)}), bf16[64,8,128]{2,1,0:T(8,128)(2,1)S(1)}, u32[]{:S(2)}, u32[]{:S(2)}) async-start(bf16[64,8,128]{2,1,0:T(8,128)(2,1)} %broadcast_in_dim.12), calls=%async_computation | async-start | bytes 262144 | tf_op jit(solution)/shard_map/all_to_all | solution.py:21
  12.7 8.4 %all-to-all-done = bf16[64,8,128]{2,1,0:T(8,128)(2,1)S(1)} async-done(((bf16[64,8,128]{2,1,0:T(8,128)(2,1)}), bf16[64,8,128]{2,1,0:T(8,128)(2,1)S(1)}, u32[]{:S(2)}, u32[]{:S(2)}) %all-to-all-start) | async-done | bytes 131104 | tf_op jit(solution)/shard_map/all_to_all | solution.py:21
  23.6 14.0 %all_to_all.45 = f32[64,8,128]{2,1,0:T(8,128)S(1)} all-to-all(f32[64,8,128]{2,1,0:T(8,128)S(1)} %bitcast.57), channel_id=1, replica_groups=mesh['vox_0'=4,'vox_1'=2,'vox_2'=4,'vox_3'=2,'load'=4] {'vox_0','vox_1',..., dimensions={0} | all-to-all | bytes 524288 | tf_op jit(solution)/shard_map/all_to_all | solution.py:37
  39.0 4.6 %all-to-all-start.2 = ((f32[64,8,128]{2,1,0:T(8,128)}), f32[64,8,128]{2,1,0:T(8,128)S(1)}, u32[]{:S(2)}, u32[]{:S(2)}) async-start(f32[64,8,128]{2,1,0:T(8,128)} %broadcast_in_dim.13), calls=%async_computation.2 | async-start | bytes 524288 | tf_op jit(solution)/shard_map/all_to_all | solution.py:21
  43.7 9.8 %all-to-all-done.2 = f32[64,8,128]{2,1,0:T(8,128)S(1)} async-done(((f32[64,8,128]{2,1,0:T(8,128)}), f32[64,8,128]{2,1,0:T(8,128)S(1)}, u32[]{:S(2)}, u32[]{:S(2)}) %all-to-all-start.2) | async-done | bytes 262176 | tf_op jit(solution)/shard_map/all_to_all | solution.py:21
  55.1 7.4 %psum.105 = f32[]{:T(128)} all-reduce(f32[]{:T(128)} %get-tuple-element.4), channel_id=1, replica_groups=mesh['vox_0'=4,'vox_1'=2,'vox_2'=4,'vox_3'=2,'load'=4] {'vox_0'}, use_global_device_ids=true, to_apply=%region_2.0 | all-reduce | flops 1 | bytes 8 | tf_op jit(solution)/shard_map/psum | solution.py:43
  66.8 7.5 %psum.107 = f32[]{:T(128)} all-reduce(f32[]{:T(128)} %psum.106), channel_id=1, replica_groups=mesh['vox_0'=4,'vox_1'=2,'vox_2'=4,'vox_3'=2,'load'=4] {'vox_2'}, use_global_device_ids=true, to_apply=%region_4.0 | all-reduce | flops 1 | bytes 8 | tf_op jit(solution)/shard_map/psum | solution.py:43
  74.3 8.3 %psum.108 = f32[]{:T(128)} all-reduce(f32[]{:T(128)} %psum.107), channel_id=1, replica_groups=mesh['vox_0'=4,'vox_1'=2,'vox_2'=4,'vox_3'=2,'load'=4] {'vox_3'}, use_global_device_ids=true, to_apply=%region_5.0 | all-reduce | flops 1 | bytes 8 | tf_op jit(solution)/shard_map/psum | solution.py:43
  82.6 12.6 %psum.109 = f32[]{:T(128)} all-reduce(f32[]{:T(128)} %psum.108), channel_id=1, replica_groups=mesh['vox_0'=4,'vox_1'=2,'vox_2'=4,'vox_3'=2,'load'=4] {'load'}, use_global_device_ids=true, to_apply=%region_6.0 | all-reduce | flops 1 | bytes 8 | tf_op jit(solution)/shard_map/psum | solution.py:43
  95.9 14.2 %all_to_all.46 = bf16[64,8,128]{2,1,0:T(8,128)(2,1)S(1)} all-to-all(bf16[64,8,128]{2,1,0:T(8,128)(2,1)S(1)} %broadcast_in_dim.14), channel_id=1, replica_groups=mesh['vox_0'=4,'vox_1'=2,'vox_2'=4,'vox_3'=2,'load'=4] {'vox_0','vox_1',..., dimensions={0} | all-to-all | bytes 262144 | tf_op jit(solution)/shard_map/all_to_all | solution.py:21
  112.6 14.0 %all_to_all.47 = f32[64,8,128]{2,1,0:T(8,128)S(1)} all-to-all(f32[64,8,128]{2,1,0:T(8,128)S(1)} %bitcast.58), channel_id=1, replica_groups=mesh['vox_0'=4,'vox_1'=2,'vox_2'=4,'vox_3'=2,'load'=4] {'vox_0','vox_1',..., dimensions={0} | all-to-all | bytes 524288 | tf_op jit(solution)/shard_map/all_to_all | solution.py:37
  126.7 14.2 %all_to_all.48 = f32[64,8,128]{2,1,0:T(8,128)S(1)} all-to-all(f32[64,8,128]{2,1,0:T(8,128)S(1)} %broadcast_in_dim.15), channel_id=1, replica_groups=mesh['vox_0'=4,'vox_1'=2,'vox_2'=4,'vox_3'=2,'load'=4] {'vox_0','vox_1',..., dimensions={0} | all-to-all | bytes 524288 | tf_op jit(solution)/shard_map/all_to_all | solution.py:21
  142.5 7.4 %psum.110 = f32[]{:T(128)} all-reduce(f32[]{:T(128)} %get-tuple-element.6), channel_id=1, replica_groups=mesh['vox_0'=4,'vox_1'=2,'vox_2'=4,'vox_3'=2,'load'=4] {'vox_0'}, use_global_device_ids=true, to_apply=%region_9.0 | all-reduce | flops 1 | bytes 8 | tf_op jit(solution)/shard_map/psum | solution.py:43
  149.9 4.4 %psum.111 = f32[]{:T(128)} all-reduce(f32[]{:T(128)} %psum.110), channel_id=1, replica_groups=mesh['vox_0'=4,'vox_1'=2,'vox_2'=4,'vox_3'=2,'load'=4] {'vox_1'}, use_global_device_ids=true, to_apply=%region_10.0 | all-reduce | flops 1 | bytes 8 | tf_op jit(solution)/shard_map/psum | solution.py:43
  154.3 7.5 %psum.112 = f32[]{:T(128)} all-reduce(f32[]{:T(128)} %psum.111), channel_id=1, replica_groups=mesh['vox_0'=4,'vox_1'=2,'vox_2'=4,'vox_3'=2,'load'=4] {'vox_2'}, use_global_device_ids=true, to_apply=%region_11.0 | all-reduce | flops 1 | bytes 8 | tf_op jit(solution)/shard_map/psum | solution.py:43
  161.7 8.3 %psum.113 = f32[]{:T(128)} all-reduce(f32[]{:T(128)} %psum.112), channel_id=1, replica_groups=mesh['vox_0'=4,'vox_1'=2,'vox_2'=4,'vox_3'=2,'load'=4] {'vox_3'}, use_global_device_ids=true, to_apply=%region_12.0 | all-reduce | flops 1 | bytes 8 | tf_op jit(solution)/shard_map/psum | solution.py:43
  170.1 8.7 %psum.114 = f32[]{:T(128)} all-reduce(f32[]{:T(128)} %psum.113), channel_id=1, replica_groups=mesh['vox_0'=4,'vox_1'=2,'vox_2'=4,'vox_3'=2,'load'=4] {'load'}, use_global_device_ids=true, to_apply=%region_13.0 | all-reduce | flops 1 | bytes 8 | tf_op jit(solution)/shard_map/psum | solution.py:43
  179.4 14.2 %all_to_all.49 = bf16[64,8,128]{2,1,0:T(8,128)(2,1)S(1)} all-to-all(bf16[64,8,128]{2,1,0:T(8,128)(2,1)S(1)} %broadcast_in_dim.16), channel_id=1, replica_groups=mesh['vox_0'=4,'vox_1'=2,'vox_2'=4,'vox_3'=2,'load'=4] {'vox_0','vox_1',..., dimensions={0} | all-to-all | bytes 262144 | tf_op jit(solution)/shard_map/all_to_all | solution.py:21
  196.4 14.0 %all_to_all.50 = f32[64,8,128]{2,1,0:T(8,128)S(1)} all-to-all(f32[64,8,128]{2,1,0:T(8,128)S(1)} %bitcast.59), channel_id=1, replica_groups=mesh['vox_0'=4,'vox_1'=2,'vox_2'=4,'vox_3'=2,'load'=4] {'vox_0','vox_1',..., dimensions={0} | all-to-all | bytes 524288 | tf_op jit(solution)/shard_map/all_to_all | solution.py:37
  210.5 14.1 %all_to_all.51 = f32[64,8,128]{2,1,0:T(8,128)S(1)} all-to-all(f32[64,8,128]{2,1,0:T(8,128)S(1)} %broadcast_in_dim.17), channel_id=1, replica_groups=mesh['vox_0'=4,'vox_1'=2,'vox_2'=4,'vox_3'=2,'load'=4] {'vox_0','vox_1',..., dimensions={0} | all-to-all | bytes 524288 | tf_op jit(solution)/shard_map/all_to_all | solution.py:21
  226.2 7.4 %psum.115 = f32[]{:T(128)} all-reduce(f32[]{:T(128)} %get-tuple-element.8), channel_id=1, replica_groups=mesh['vox_0'=4,'vox_1'=2,'vox_2'=4,'vox_3'=2,'load'=4] {'vox_0'}, use_global_device_ids=true, to_apply=%region_16.0 | all-reduce | flops 1 | bytes 8 | tf_op jit(solution)/shard_map/psum | solution.py:43
  238.0 7.5 %psum.117 = f32[]{:T(128)} all-reduce(f32[]{:T(128)} %psum.116), channel_id=1, replica_groups=mesh['vox_0'=4,'vox_1'=2,'vox_2'=4,'vox_3'=2,'load'=4] {'vox_2'}, use_global_device_ids=true, to_apply=%region_18.0 | all-reduce | flops 1 | bytes 8 | tf_op jit(solution)/shard_map/psum | solution.py:43
  245.5 8.3 %psum.118 = f32[]{:T(128)} all-reduce(f32[]{:T(128)} %psum.117), channel_id=1, replica_groups=mesh['vox_0'=4,'vox_1'=2,'vox_2'=4,'vox_3'=2,'load'=4] {'vox_3'}, use_global_device_ids=true, to_apply=%region_19.0 | all-reduce | flops 1 | bytes 8 | tf_op jit(solution)/shard_map/psum | solution.py:43
  253.8 8.7 %psum.119 = f32[]{:T(128)} all-reduce(f32[]{:T(128)} %psum.118), channel_id=1, replica_groups=mesh['vox_0'=4,'vox_1'=2,'vox_2'=4,'vox_3'=2,'load'=4] {'load'}, use_global_device_ids=true, to_apply=%region_20.0 | all-reduce | flops 1 | bytes 8 | tf_op jit(solution)/shard_map/psum | solution.py:43
  (55 shorter events, 24.9 us)
Async XLA Ops:
  0.6 20.4 %copy-start = (bf16[1024,512]{1,0:T(8,128)(2,1)S(1)}, bf16[1024,512]{1,0:T(8,128)(2,1)}, u32[]{:S(2)}) copy-start(bf16[1024,512]{1,0:T(8,128)(2,1)} %param.11) | copy-start | bytes 3145732
  2.1 10.5 %copy-start.4 = (f32[1024]{0:T(1024)S(1)}, f32[1024]{0:T(1024)}, u32[]{:S(2)}) copy-start(f32[1024]{0:T(1024)} %param.12) | copy-start | bytes 12292
  2.1 10.5 %copy-start.6 = (f32[1024]{0:T(1024)S(1)}, f32[1024]{0:T(1024)}, u32[]{:S(2)}) copy-start(f32[1024]{0:T(1024)} %param.13) | copy-start | bytes 12292
  2.1 19.0 %all-to-all-start = ((bf16[64,8,128]{2,1,0:T(8,128)(2,1)}), bf16[64,8,128]{2,1,0:T(8,128)(2,1)S(1)}, u32[]{:S(2)}, u32[]{:S(2)}) async-start(bf16[64,8,128]{2,1,0:T(8,128)(2,1)} %broadcast_in_dim.12), calls=%async_computation | async-start | bytes 262144 | tf_op jit(solution)/shard_map/all_to_all | solution.py:21
  12.6 8.5 %copy-start.5 = (f32[1024]{0:T(1024)S(1)}, f32[1024]{0:T(1024)}, u32[]{:S(2)}) copy-start(f32[1024]{0:T(1024)} %param.15) | copy-start | bytes 12292
  12.6 8.5 %copy-start.7 = (f32[128]{0:T(128)S(1)}, f32[128]{0:T(128)}, u32[]{:S(2)}) copy-start(f32[128]{0:T(128)} %param.16) | copy-start | bytes 1540
  12.6 9.9 %copy-start.8 = (s32[1024,128]{1,0:T(8,128)S(1)}, s32[1024,128]{1,0:T(8,128)}, u32[]{:S(2)}) copy-start(s32[1024,128]{1,0:T(8,128)} %param.17) | copy-start | bytes 1572868
  12.6 9.9 %copy-start.9 = (f32[1024]{0:T(1024)S(1)}, f32[1024]{0:T(1024)}, u32[]{:S(2)}) copy-start(f32[1024]{0:T(1024)} %param.14) | copy-start | bytes 12292
  37.6 0.7 copy-start.2
  39.0 71.2 %copy-start.1 = (f32[1024,128]{1,0:T(8,128)S(1)}, f32[1024,128]{1,0:T(8,128)}, u32[]{:S(2)}) copy-start(f32[1024,128]{1,0:T(8,128)} %param.18) | copy-start | bytes 1572868
  39.0 14.5 %all-to-all-start.2 = ((f32[64,8,128]{2,1,0:T(8,128)}), f32[64,8,128]{2,1,0:T(8,128)S(1)}, u32[]{:S(2)}, u32[]{:S(2)}) async-start(f32[64,8,128]{2,1,0:T(8,128)} %broadcast_in_dim.13), calls=%async_computation.2 | async-start | bytes 524288 | tf_op jit(solution)/shard_map/all_to_all | solution.py:21
  82.6 13.3 %copy-start.3 = (f32[8,128]{1,0:T(8,128)S(1)}, f32[8,128]{1,0:T(8,128)}, u32[]{:S(2)}) copy-start(f32[8,128]{1,0:T(8,128)} %param.19) | copy-start | bytes 12292
  110.8 0.8 copy-start.10
  126.7 67.0 %copy-start.11 = (f32[1024,128]{1,0:T(8,128)S(1)}, f32[1024,128]{1,0:T(8,128)}, u32[]{:S(2)}) copy-start(f32[1024,128]{1,0:T(8,128)} %copy-done.10) | copy-start | bytes 1572868
where the time goes:
time: 265 us; the launch traced here: 264 us
  blocking collectives  211 us (80%)
  waiting for transfers between devices  18.3 us (7%)
  starting transfers between devices  15.1 us (6%)
  matrix products  11.2 us (4%)
  local copies, waits for them, and re-layouts  3.33 us (1%)
  between operations  2.82 us (1%)
    psum x15, blocking collectives, over_axes(): shard = lax.psum(shard, axis)  113 us
    all_to_all x4, blocking collectives, from_everyone(): lax.all_to_all(jnp.broadcast_to(shard[None], (size, *shard.shape)), axis,...  56.7 us
    all_to_all x3, blocking collectives, sum_at_owner(): pieces = lax.all_to_all(in_blocks(shard, dim, size), axis, 0, 0, tiled=True)  42 us
    all_to_all x2, waiting for transfers between devices, from_everyone(): lax.all_to_all(jnp.broadcast_to(shard[None], (size, *shard.shape)), axis,...  18.3 us
    all_to_all x2, starting transfers between devices, from_everyone(): lax.all_to_all(jnp.broadcast_to(shard[None], (size, *shard.shape)), axis,...  15.1 us
  transfers between devices with their start and end apart: 2, of which 2 were waited for; matrix products, arithmetic and copies ran while one was open for 0% of the time, Pallas kernels for 0%

commit v1 on v0

v1 whole, which is shorter than its diff:
```python
import jax
import jax.numpy as jnp
from jax import lax
from jax.sharding import Mesh
from jax.sharding import PartitionSpec as P

M = 512
ITERS = 3
VOX = ("x", "zl", "y", "core")
XY = ("x", "y")
RING = ("zl", "load")
SWAP = [(0, 1), (1, 0)]
CHUNK = 16


def split_two(value):
    high = lax.reduce_precision(value, 8, 7)
    return high.astype(jnp.bfloat16), (value - high).astype(jnp.bfloat16)


def dot(a, b, dims):
    return lax.dot_general(a, b, (dims, ((), ())), preferred_element_type=jnp.float32)


def to_everyone(block, axes):
    size = lax.axis_size(axes)
    return lax.all_to_all(
        jnp.broadcast_to(block[None], (size, *block.shape)), axes, 0, 0, tiled=True
    )


def shards(
    reduced_shape_matrix,
    young_modulus,
    work_stiffening_modulus,
    entry_flow_stress,
    dilation_factor,
    heat_difference,
    flowing_entry_flags,
    starting_permanent_deformation,
    starting_weights,
    applied_reduced_vector,
    approx_tangent_inverse,
):
    own_rows, points = starting_weights.shape
    entries = M * points * lax.axis_size("load")
    vox = lax.axis_index(VOX)
    core = lax.axis_index("core")
    load = lax.axis_index("load")
    plastic = starting_permanent_deformation
    active = flowing_entry_flags.astype(jnp.float32)
    modulus = young_modulus[:, None]
    harden = work_stiffening_modulus[:, None]
    yielded = entry_flow_stress[:, None]
    heating_history = dilation_factor[:, None] * heat_difference[None, :]

    xi = to_everyone(starting_weights, VOX).reshape(M, points)

    inverse_high, inverse_low = split_two(approx_tangent_inverse)
    both = dot(inverse_high, reduced_shape_matrix, ((1,), (1,))) + dot(
        inverse_low, reduced_shape_matrix, ((1,), (1,))
    )
    map_high, map_low = split_two(both)
    applied = lax.dynamic_update_slice_in_dim(
        jnp.zeros((M, points), jnp.float32), applied_reduced_vector, vox * own_rows, 0
    )
    applied = jnp.dot(approx_tangent_inverse, applied, precision=lax.Precision.HIGHEST)

    for sweep in range(ITERS):
        strain = dot(reduced_shape_matrix, xi.astype(jnp.bfloat16), ((1,), (0,)))
        trial = modulus * (strain - heating_history - plastic)
        excess = trial - yielded * jnp.tanh(trial / yielded)
        increment = active * excess / (modulus + harden)
        stress = (trial - modulus * increment).astype(jnp.bfloat16)
        plastic = plastic + increment
        partial = dot(map_high, stress, ((1,), (0,))) + dot(map_low, stress, ((1,), (0,))) - applied
        halves = partial.reshape(-1, 2, CHUNK, points)
        kept = lax.dynamic_index_in_dim(halves, core, 1, False)
        given = lax.dynamic_index_in_dim(halves, 1 - core, 1, False)
        kept = kept + lax.ppermute(given, "core", SWAP)
        chunk = jnp.sum(lax.all_to_all(kept, XY, 0, 0, tiled=True), axis=0)
        ring = to_everyone(chunk, RING)
        ring = jnp.sum(ring.reshape(2, -1, CHUNK, points), axis=0)
        squares = jnp.sum(ring * ring)
        delta = lax.dynamic_index_in_dim(ring, load, 0, False)
        message = jnp.concatenate([delta, jnp.full((8, points), squares)], axis=0)
        other = lax.ppermute(message, "core", SWAP)
        pair = jnp.where(core == 0, jnp.stack([message, other]), jnp.stack([other, message]))
        pairs = to_everyone(pair, XY)
        delta = pairs[:, :, :CHUNK].reshape(M, points)
        spread = jnp.sum(pairs[:, :, CHUNK, 0]) / entries
        xi = xi - delta / (1.0 + spread)
    return (lax.dynamic_slice_in_dim(xi, vox * own_rows, own_rows, 0), plastic)


def solution(mesh):
    split = Mesh(
        mesh.devices.reshape(4, 2, 4, 2, mesh.shape["load"]),
        ("x", "zl", "y", "core", "load"),
    )
    return jax.shard_map(
        shards,
        mesh=split,
        in_specs=(
            P(VOX, None),
            P(VOX),
            P(VOX),
            P(VOX),
            P(VOX),
            P("load"),
            P(VOX, "load"),
            P(VOX, "load"),
            P(VOX, "load"),
            P(VOX, "load"),
            P(),
        ),
        out_specs=(P(VOX, "load"), P(VOX, "load")),
        check_vma=False,
    )
```

time: 265 us -> 171 us (0.65)
  blocking collectives: 211 us -> 85.2 us
  starting transfers between devices: 15.1 us -> 30.2 us
  other arithmetic: 1.63 us -> 10 us
  local copies, waits for them, and re-layouts: 3.33 us -> 8.86 us
  matrix products: 11.2 us -> 16 us
    psum x15 -> x0, blocking collectives: 113 us -> none  [over_axes(): shard = lax.psum(shard, axis)]
    all_to_all x7 -> x8, blocking collectives: 98.7 us -> 85.2 us  [the longest x5 55.4 us: to_everyone(): lax.all_to_all(jnp.broadcast_to(block[None], (size, *block.shape)), axes,...]
    ppermute x0 -> x6, starting transfers between devices: none -> 12.6 us  [the longest x3 8.99 us: shards(): other = lax.ppermute(message, 'core', SWAP)]
    all_to_all x2, waiting for transfers between devices: 18.3 us -> 11.1 us  [to_everyone(): lax.all_to_all(jnp.broadcast_to(block[None], (size, *block.shape)), axes,...]
    ppermute x0 -> x6, waiting for transfers between devices: none -> 5.67 us  [the longest x3 3.17 us: shards(): kept = kept + lax.ppermute(given, 'core', SWAP)]
    dot_general x9 -> x12, matrix products: 11.2 us -> 16 us  [the longest x11 14.3 us: dot(): lax.dot_general(a, b, (dims, ((), ())), preferred_element_type=jnp.float32)]
    reduce_sum x3 -> x12, other arithmetic: 0.21 us -> 3.98 us  [the longest x3 2 us: shards(): spread = jnp.sum(pairs[:, :, CHUNK, 0]) / entries]
  transfers between devices with their start and end apart: 2 -> 8, of which waited for: 2 -> 8; matrix products, arithmetic and copies ran while one was open for 0% -> 3% of each run, Pallas kernels for 0% -> 0%
where the time goes in v1:
time: 171 us; the launch traced here: 170 us
  blocking collectives  85.2 us (50%)
  starting transfers between devices  30.2 us (18%)
  waiting for transfers between devices  16.8 us (10%)
  matrix products  16 us (9%)
  other arithmetic  10 us (6%)
  local copies, waits for them, and re-layouts  8.86 us (5%)
  between operations  3.08 us (2%)
    all_to_all x5, blocking collectives, to_everyone(): lax.all_to_all(jnp.broadcast_to(block[None], (size, *block.shape)), axes,...  55.4 us
    all_to_all x3, blocking collectives, shards(): chunk = jnp.sum(lax.all_to_all(kept, XY, 0, 0, tiled=True), axis=0)  29.7 us
    all_to_all x2, starting transfers between devices, to_everyone(): lax.all_to_all(jnp.broadcast_to(block[None], (size, *block.shape)), axes,...  17.6 us
    dot_general x11, matrix products, dot(): lax.dot_general(a, b, (dims, ((), ())), preferred_element_type=jnp.float32)  14.3 us
    all_to_all x2, waiting for transfers between devices, to_everyone(): lax.all_to_all(jnp.broadcast_to(block[None], (size, *block.shape)), axes,...  11.1 us
    ppermute x3, starting transfers between devices, shards(): other = lax.ppermute(message, 'core', SWAP)  8.99 us
    unnamed x50, local copies, waits for them, and re-layouts  3.97 us
    ppermute x3, starting transfers between devices, shards(): kept = kept + lax.ppermute(given, 'core', SWAP)  3.6 us
  transfers between devices with their start and end apart: 8, of which 8 were waited for; matrix products, arithmetic and copies ran while one was open for 3% of the time, Pallas kernels for 0%

profile of v1, /device:TPU:1, one launch (start us, length us, event | category | flops | bytes accessed | tf_op | source)
XLA Modules:
  0.0 170.1 jit_solution(12305454440424639260)
XLA Ops:
  0.6 1.5 broadcast_in_dim.16
  2.1 10.3 %all-to-all-start = ((f32[64,8,128]{2,1,0:T(8,128)}), f32[64,8,128]{2,1,0:T(8,128)S(1)}, u32[]{:S(2)}, u32[]{:S(2)}) async-start(f32[64,8,128]{2,1,0:T(8,128)} %broadcast_in_dim.16), calls=%async_computation | async-start | bytes 524288 | tf_op jit(solution)/shard_map/all_to_all | solution.py:27
  13.2 2.1 %fusion.14 = f32[512,1024]{1,0:T(8,128)S(1)} fusion(bf16[1024,512]{1,0:T(8,128)(2,1)S(1)} %copy-done, f32[512,512]{1,0:T(8,128)} %param.21), kind=kOutput, calls=%fused_computation.25 | convolution fusion | flops 537395200 | bytes 4194304 | tf_op jit(solution)/shard_map/dot_general | solution.py:22
  15.3 1.7 %convolution_bitcast_fusion.2 = f32[512,128]{1,0:T(8,128)} fusion(f32[512,128]{1,0:T(8,128)S(1)} %constant_dynamic-update-slice_fusion, f32[512,512]{1,0:T(8,128)S(1)} %copy-done.1), kind=kOutput, calls=%fused_computation.17 | convolution fusion | flops 402653184 | bytes 1572864 | tf_op jit(solution)/shard_map/dot_general | solution.py:67
  17.9 4.4 %all-to-all-done = f32[64,8,128]{2,1,0:T(8,128)S(1)} async-done(((f32[64,8,128]{2,1,0:T(8,128)}), f32[64,8,128]{2,1,0:T(8,128)S(1)}, u32[]{:S(2)}, u32[]{:S(2)}) %all-to-all-start) | async-done | bytes 262176 | tf_op jit(solution)/shard_map/all_to_all | solution.py:27
  22.3 2.7 %subtract_convert_fusion.2 = (bf16[1024,128]{1,0:T(8,128)(2,1)S(1)}, f32[1024,128]{1,0:T(8,128)}) fusion(f32[1024]{0:T(1024)S(1)} %copy-done.11, f32[1024]{0:T(1024)S(1)} %add.83, f32[1024]{0:T(1024)S(1)} %copy-done.22, s32[1024,128]{1,0:T(8,128)} %param.17, f32[1024,128]{1,0:T(8,128)} %param.18, f32[128]{0:T(128)S(1)} %copy-done.17, ...), kind=kOutput, calls=%fused_computation.30 | convolution fusion | flops 135921664 | bytes 3162624 | tf_op jit(solution)/shard_map/dot_general | solution.py:22
  30.3 9.9 %all_to_all.50 = f32[16,16,128]{2,1,0:T(8,128)S(1)} all-to-all(f32[16,16,128]{2,1,0:T(8,128)S(1)} %bitcast_add_fusion.2), channel_id=1, replica_groups=mesh['x'=4,'zl'=2,'y'=4,'core'=2,'load'=4] {'x','y'}, dimensions={0} | all-to-all | bytes 262144 | tf_op jit(solution)/shard_map/all_to_all | solution.py:81
  40.8 7.3 %all-to-all-start.2 = ((f32[8,16,128]{2,1,0:T(8,128)}), f32[8,16,128]{2,1,0:T(8,128)S(1)}, u32[]{:S(2)}, u32[]{:S(2)}) async-start(f32[8,16,128]{2,1,0:T(8,128)} %broadcast_in_dim.18), calls=%async_computation.2 | async-start | bytes 131072 | tf_op jit(solution)/shard_map/all_to_all | solution.py:27
  48.1 6.7 %all-to-all-done.2 = f32[8,16,128]{2,1,0:T(8,128)S(1)} async-done(((f32[8,16,128]{2,1,0:T(8,128)}), f32[8,16,128]{2,1,0:T(8,128)S(1)}, u32[]{:S(2)}, u32[]{:S(2)}) %all-to-all-start.2) | async-done | bytes 65568 | tf_op jit(solution)/shard_map/all_to_all | solution.py:27
  56.1 3.2 %collective-permute-start.1 = (f32[24,128]{1,0:T(8,128)S(1)}, f32[24,128]{1,0:T(8,128)S(1)}, u32[]{:S(2)}, u32[]{:S(2)}) collective-permute-start(f32[24,128]{1,0:T(8,128)S(1)} %get-tuple-element.9), channel_id=1, source_target_pairs={{0,4},{4,0},{1,5},{5,1},{2,6},{6,2},{3,7},{7,3},{8,12},{12,8},{9,1... | collective-permute-start | bytes 36872 | tf_op jit(solution)/shard_map/ppermute | solution.py:87
  60.2 12.4 %all_to_all.51 = f32[16,2,24,128]{3,2,1,0:T(8,128)S(1)} all-to-all(f32[16,2,24,128]{3,2,1,0:T(8,128)S(1)} %broadcast_in_dim.19), channel_id=1, replica_groups=mesh['x'=4,'zl'=2,'y'=4,'core'=2,'load'=4] {'x','y'}, dimensions={0} | all-to-all | bytes 786432 | tf_op jit(solution)/shard_map/all_to_all | solution.py:27
  76.5 1.6 fusion.8
  80.2 1.6 collective-permute-start.2
  82.8 9.9 %all_to_all.52 = f32[16,16,128]{2,1,0:T(8,128)S(1)} all-to-all(f32[16,16,128]{2,1,0:T(8,128)S(1)} %bitcast_add_fusion.1), channel_id=1, replica_groups=mesh['x'=4,'zl'=2,'y'=4,'core'=2,'load'=4] {'x','y'}, dimensions={0} | all-to-all | bytes 262144 | tf_op jit(solution)/shard_map/all_to_all | solution.py:81
  92.8 9.1 %all_to_all.53 = f32[8,16,128]{2,1,0:T(8,128)S(1)} all-to-all(f32[8,16,128]{2,1,0:T(8,128)S(1)} %broadcast_in_dim.20), channel_id=1, replica_groups=mesh['x'=4,'zl'=2,'y'=4,'core'=2,'load'=4] {'zl','load'}, dimensions={0} | all-to-all | bytes 131072 | tf_op jit(solution)/shard_map/all_to_all | solution.py:27
  103.3 2.9 %collective-permute-start.3 = (f32[24,128]{1,0:T(8,128)S(1)}, f32[24,128]{1,0:T(8,128)S(1)}, u32[]{:S(2)}, u32[]{:S(2)}) collective-permute-start(f32[24,128]{1,0:T(8,128)S(1)} %get-tuple-element.7), channel_id=1, source_target_pairs={{0,4},{4,0},{1,5},{5,1},{2,6},{6,2},{3,7},{7,3},{8,12},{12,8},{9,1... | collective-permute-start | bytes 36872 | tf_op jit(solution)/shard_map/ppermute | solution.py:87
  107.1 12.4 %all_to_all.54 = f32[16,2,24,128]{3,2,1,0:T(8,128)S(1)} all-to-all(f32[16,2,24,128]{3,2,1,0:T(8,128)S(1)} %broadcast_in_dim.21), channel_id=1, replica_groups=mesh['x'=4,'zl'=2,'y'=4,'core'=2,'load'=4] {'x','y'}, dimensions={0} | all-to-all | bytes 786432 | tf_op jit(solution)/shard_map/all_to_all | solution.py:27
  123.6 3.1 %add_add_fusion = (f32[1024,128]{1,0:T(8,128)}, f32[1024,128]{1,0:T(8,128)S(1)}) fusion(f32[1024,128]{1,0:T(8,128)} %param.18, f32[1024,128]{1,0:T(8,128)} %get-tuple-element.3, f32[1024]{0:T(1024)S(1)} %copy-done.15, f32[1024]{0:T(1024)S(1)} %copy-done.24, s32[1024,128]{1,0:T(8,128)} %param.17, f32[1024,128]{1,0:T(8,128)} %copy-done.9, ...), kind=kOutput, calls=%fused_computation.38 | convolution fusion | flops 136642560 | bytes 4473344 | tf_op jit(solution)/shard_map/dot_general | solution.py:22
  128.4 1.6 collective-permute-start.4
  131.0 9.9 %all_to_all.55 = f32[16,16,128]{2,1,0:T(8,128)S(1)} all-to-all(f32[16,16,128]{2,1,0:T(8,128)S(1)} %bitcast_add_fusion), channel_id=1, replica_groups=mesh['x'=4,'zl'=2,'y'=4,'core'=2,'load'=4] {'x','y'}, dimensions={0} | all-to-all | bytes 262144 | tf_op jit(solution)/shard_map/all_to_all | solution.py:81
  141.0 9.1 %all_to_all.56 = f32[8,16,128]{2,1,0:T(8,128)S(1)} all-to-all(f32[8,16,128]{2,1,0:T(8,128)S(1)} %broadcast_in_dim.22), channel_id=1, replica_groups=mesh['x'=4,'zl'=2,'y'=4,'core'=2,'load'=4] {'zl','load'}, dimensions={0} | all-to-all | bytes 131072 | tf_op jit(solution)/shard_map/all_to_all | solution.py:27
  151.4 2.9 %collective-permute-start.5 = (f32[24,128]{1,0:T(8,128)S(1)}, f32[24,128]{1,0:T(8,128)S(1)}, u32[]{:S(2)}, u32[]{:S(2)}) collective-permute-start(f32[24,128]{1,0:T(8,128)S(1)} %get-tuple-element.5), channel_id=1, source_target_pairs={{0,4},{4,0},{1,5},{5,1},{2,6},{6,2},{3,7},{7,3},{8,12},{12,8},{9,1... | collective-permute-start | bytes 36872 | tf_op jit(solution)/shard_map/ppermute | solution.py:87
  155.2 12.4 %all_to_all.57 = f32[16,2,24,128]{3,2,1,0:T(8,128)S(1)} all-to-all(f32[16,2,24,128]{3,2,1,0:T(8,128)S(1)} %broadcast_in_dim.23), channel_id=1, replica_groups=mesh['x'=4,'zl'=2,'y'=4,'core'=2,'load'=4] {'x','y'}, dimensions={0} | all-to-all | bytes 786432 | tf_op jit(solution)/shard_map/all_to_all | solution.py:27
  168.9 1.3 dynamic-slice_subtract_fusion
  (105 shorter events, 27.0 us)
Async XLA Ops:
  0.6 12.6 %copy-start = (bf16[1024,512]{1,0:T(8,128)(2,1)S(1)}, bf16[1024,512]{1,0:T(8,128)(2,1)}, u32[]{:S(2)}) copy-start(bf16[1024,512]{1,0:T(8,128)(2,1)} %param.11) | copy-start | bytes 3145732
  2.1 20.1 %all-to-all-start = ((f32[64,8,128]{2,1,0:T(8,128)}), f32[64,8,128]{2,1,0:T(8,128)S(1)}, u32[]{:S(2)}, u32[]{:S(2)}) async-start(f32[64,8,128]{2,1,0:T(8,128)} %broadcast_in_dim.16), calls=%async_computation | async-start | bytes 524288 | tf_op jit(solution)/shard_map/all_to_all | solution.py:27
  13.2 9.1 %copy-start.13 = (f32[1024]{0:T(1024)}, f32[1024]{0:T(1024)S(1)}, u32[]{:S(2)}) copy-start(f32[1024]{0:T(1024)S(1)} %add.83) | copy-start | bytes 12292
  13.2 2.1 %copy-start.1 = (f32[512,512]{1,0:T(8,128)S(1)}, f32[512,512]{1,0:T(8,128)}, u32[]{:S(2)}) copy-start(f32[512,512]{1,0:T(8,128)} %param.21) | copy-start | bytes 3145732
  17.1 5.2 %copy-start.11 = (f32[1024]{0:T(1024)S(1)}, f32[1024]{0:T(1024)}, u32[]{:S(2)}) copy-start(f32[1024]{0:T(1024)} %param.12) | copy-start | bytes 12292
  17.1 5.2 %copy-start.12 = (f32[1024]{0:T(1024)S(1)}, f32[1024]{0:T(1024)}, u32[]{:S(2)}) copy-start(f32[1024]{0:T(1024)} %param.15) | copy-start | bytes 12292
  17.1 5.2 %copy-start.17 = (f32[128]{0:T(128)S(1)}, f32[128]{0:T(128)}, u32[]{:S(2)}) copy-start(f32[128]{0:T(128)} %param.16) | copy-start | bytes 1540
  17.1 5.2 %copy-start.22 = (f32[1024]{0:T(1024)S(1)}, f32[1024]{0:T(1024)}, u32[]{:S(2)}) copy-start(f32[1024]{0:T(1024)} %param.14) | copy-start | bytes 12292
  27.8 1.6 collective-permute-start
  40.2 36.4 %copy-start.18 = (f32[128]{0:T(128)S(1)}, f32[128]{0:T(128)}, u32[]{:S(2)}) copy-start(f32[128]{0:T(128)} %param.16) | copy-start | bytes 1540
  40.8 14.0 %all-to-all-start.2 = ((f32[8,16,128]{2,1,0:T(8,128)}), f32[8,16,128]{2,1,0:T(8,128)S(1)}, u32[]{:S(2)}, u32[]{:S(2)}) async-start(f32[8,16,128]{2,1,0:T(8,128)} %broadcast_in_dim.18), calls=%async_computation.2 | async-start | bytes 131072 | tf_op jit(solution)/shard_map/all_to_all | solution.py:27
  56.1 4.1 %collective-permute-start.1 = (f32[24,128]{1,0:T(8,128)S(1)}, f32[24,128]{1,0:T(8,128)S(1)}, u32[]{:S(2)}, u32[]{:S(2)}) collective-permute-start(f32[24,128]{1,0:T(8,128)S(1)} %get-tuple-element.9), channel_id=1, source_target_pairs={{0,4},{4,0},{1,5},{5,1},{2,6},{6,2},{3,7},{7,3},{8,12},{12,8},{9,1... | collective-permute-start | bytes 36872 | tf_op jit(solution)/shard_map/ppermute | solution.py:87
  73.3 4.9 %copy-start.14 = (f32[1024]{0:T(1024)S(1)}, f32[1024]{0:T(1024)}, u32[]{:S(2)}) copy-start(f32[1024]{0:T(1024)} %copy-done.13) | copy-start | bytes 12292
  73.3 4.9 %copy-start.23 = (f32[1024]{0:T(1024)S(1)}, f32[1024]{0:T(1024)}, u32[]{:S(2)}) copy-start(f32[1024]{0:T(1024)} %param.14) | copy-start | bytes 12292
  74.7 3.5 %copy-start.20 = (s32[1024,128]{1,0:T(8,128)S(1)}, s32[1024,128]{1,0:T(8,128)}, u32[]{:S(2)}) copy-start(s32[1024,128]{1,0:T(8,128)} %param.17) | copy-start | bytes 1572868
  80.2 2.6 %collective-permute-start.2 = (f32[16,16,128]{2,1,0:T(8,128)S(1)}, f32[16,16,128]{2,1,0:T(8,128)S(1)}, u32[]{:S(2)}, u32[]{:S(2)}) collective-permute-start(f32[16,16,128]{2,1,0:T(8,128)S(1)} %dynamic-slice_bitcast_fusion.1), channel_id=1, source_target_pairs={{0,4},{4,0},{1,5},{5,1},{2,6},{6,2},{3,7},{7,3},{8,12},{12,8},{9,1... | collective-permute-start | bytes 393224 | tf_op jit(solution)/shard_map/ppermute | solution.py:80
  92.8 30.7 %copy-start.15 = (f32[1024]{0:T(1024)S(1)}, f32[1024]{0:T(1024)}, u32[]{:S(2)}) copy-start(f32[1024]{0:T(1024)} %copy-done.13) | copy-start | bytes 12292
  92.8 30.7 %copy-start.19 = (f32[128]{0:T(128)S(1)}, f32[128]{0:T(128)}, u32[]{:S(2)}) copy-start(f32[128]{0:T(128)} %param.16) | copy-start | bytes 1540
  92.8 30.7 %copy-start.24 = (f32[1024]{0:T(1024)S(1)}, f32[1024]{0:T(1024)}, u32[]{:S(2)}) copy-start(f32[1024]{0:T(1024)} %param.14) | copy-start | bytes 12292
  103.3 3.7 %collective-permute-start.3 = (f32[24,128]{1,0:T(8,128)S(1)}, f32[24,128]{1,0:T(8,128)S(1)}, u32[]{:S(2)}, u32[]{:S(2)}) collective-permute-start(f32[24,128]{1,0:T(8,128)S(1)} %get-tuple-element.7), channel_id=1, source_target_pairs={{0,4},{4,0},{1,5},{5,1},{2,6},{6,2},{3,7},{7,3},{8,12},{12,8},{9,1... | collective-permute-start | bytes 36872 | tf_op jit(solution)/shard_map/ppermute | solution.py:87
  123.5 3.1 %copy-start.10 = (f32[512,128]{1,0:T(8,128)}, f32[512,128]{1,0:T(8,128)S(1)}, u32[]{:S(2)}) copy-start(f32[512,128]{1,0:T(8,128)S(1)} %bitcast_subtract_fusion) | copy-start | bytes 786436
  123.5 3.1 %copy-start.21 = (s32[1024,128]{1,0:T(8,128)S(1)}, s32[1024,128]{1,0:T(8,128)}, u32[]{:S(2)}) copy-start(s32[1024,128]{1,0:T(8,128)} %param.17) | copy-start | bytes 1572868
  128.4 2.6 %collective-permute-start.4 = (f32[16,16,128]{2,1,0:T(8,128)S(1)}, f32[16,16,128]{2,1,0:T(8,128)S(1)}, u32[]{:S(2)}, u32[]{:S(2)}) collective-permute-start(f32[16,16,128]{2,1,0:T(8,128)S(1)} %dynamic-slice_bitcast_fusion), channel_id=1, source_target_pairs={{0,4},{4,0},{1,5},{5,1},{2,6},{6,2},{3,7},{7,3},{8,12},{12,8},{9,1... | collective-permute-start | bytes 393224 | tf_op jit(solution)/shard_map/ppermute | solution.py:80
  151.4 3.7 %collective-permute-start.5 = (f32[24,128]{1,0:T(8,128)S(1)}, f32[24,128]{1,0:T(8,128)S(1)}, u32[]{:S(2)}, u32[]{:S(2)}) collective-permute-start(f32[24,128]{1,0:T(8,128)S(1)} %get-tuple-element.5), channel_id=1, source_target_pairs={{0,4},{4,0},{1,5},{5,1},{2,6},{6,2},{3,7},{7,3},{8,12},{12,8},{9,1... | collective-permute-start | bytes 36872 | tf_op jit(solution)/shard_map/ppermute | solution.py:87
  (9 other events, 8.9 us)

commit v2 on v1

v2 whole, which is shorter than its diff:
```python
import functools

import jax
import jax.numpy as jnp
from jax import lax
from jax.experimental import pallas as pl
from jax.experimental.pallas import tpu as pltpu
from jax.sharding import Mesh
from jax.sharding import PartitionSpec as P

M = 512
ITERS = 3
VOX = ("x", "zl", "y", "core")
PLANE = ("x", "y")
COLUMNS = ("x", "y", "core")
RING = ("zl", "load")
SWAP = [(0, 1), (1, 0)]
CHUNK = 16
CHUNKS = M // CHUNK
BLOCK = 128

HERE = pl.BlockSpec(memory_space=pltpu.VMEM)
ANYWHERE = pl.BlockSpec(memory_space=pl.ANY)
SCALAR = pl.BlockSpec(memory_space=pltpu.SMEM)
F32 = jnp.float32
BF16 = jnp.bfloat16


def call(kernel, name, outs, n_scalars, n_arrays, scratch=(), n_unread=0):
    return pl.pallas_call(
        kernel,
        name=name,
        out_shape=[jax.ShapeDtypeStruct(*out) for out in outs],
        in_specs=[SCALAR] * n_scalars + [HERE] * n_arrays + [ANYWHERE] * n_unread,
        out_specs=[HERE] * len(outs),
        scratch_shapes=list(scratch),
        compiler_params=pltpu.CompilerParams(vmem_limit_bytes=16 << 20),
    )


def dot(a, b, dims=((1,), (0,))):
    return lax.dot_general(a, b, (dims, ((), ())), preferred_element_type=F32)


def split_two(value):
    high = value.astype(BF16)
    return high, (value - high.astype(F32)).astype(BF16)


def send_kernel(place, core, load, own, out):
    for peer in range(out.shape[0]):
        out[peer] = own[...]


def prepare_kernel(
    place, inverse, basis, young, harden, flow, dilate, heat, flags, applied, after,
    high_out, low_out, applied_out, young_out, flow_out, inv_flow_out, weight_out, heat_out,
    padded,
):
    inverse_high, inverse_low = split_two(inverse[...])
    for block in range(0, basis.shape[0], 256):
        rows = slice(block, block + 256)
        part = basis[rows, :]
        both = dot(inverse_high, part, ((1,), (1,))) + dot(inverse_low, part, ((1,), (1,)))
        high, low = split_two(both)
        high_out[:, rows] = high
        low_out[:, rows] = low
    padded[...] = jnp.zeros_like(padded)
    padded[pl.ds(pl.multiple_of(place[0] % 16 * 8, 8), 8), :] = applied[...]
    columns = inverse[:, pl.ds(pl.multiple_of(place[0] // 16 * 128, 128), 128)]
    a_high, a_low = split_two(columns)
    b_high, b_low = split_two(padded[...])
    applied_out[...] = dot(a_high, b_high) + (dot(a_high, b_low) + dot(a_low, b_high))
    young_t = young[...].T
    flow_t = flow[...].T
    inv_flow_t = (1.0 / flow[...]).T
    weight_t = (1.0 / (young[...] + harden[...])).T
    dilate_t = dilate[...].T
    for block in range(8):
        rows = slice(block * 128, block * 128 + 128)
        column = slice(block, block + 1)
        wide = (128, 128)
        young_out[rows, :] = jnp.broadcast_to(young_t[:, column], wide)
        flow_out[rows, :] = jnp.broadcast_to(flow_t[:, column], wide)
        inv_flow_out[rows, :] = jnp.broadcast_to(inv_flow_t[:, column], wide)
        weight_out[rows, :] = flags[rows, :].astype(F32) * weight_t[:, column]
        heat_out[rows, :] = dilate_t[:, column] * heat[...]


def factor_of(mine, other, entries):
    squares = mine[0, CHUNK:] + other[0, CHUNK:]
    for peer in range(1, mine.shape[0]):
        squares = squares + mine[peer, CHUNK:] + other[peer, CHUNK:]
    spread = jnp.sum(squares, axis=(0, 1), keepdims=True) / entries
    return 1.0 / (1.0 + spread)


def constitutive(xi_now, basis, high, low, applied, young, flow, inv_flow, weight, heat, plastic, plastic_out, sums_out, stress_all):
    for block in range(0, basis.shape[0], BLOCK):
        rows = slice(block, block + BLOCK)
        strain = dot(basis[rows, :], xi_now)
        trial = young[rows, :] * (strain - heat[rows, :] - plastic[rows, :])
        excess = trial - flow[rows, :] * jnp.tanh(trial * inv_flow[rows, :])
        increment = weight[rows, :] * excess
        plastic_out[rows, :] = plastic[rows, :] + increment
        stress_all[rows, :] = (trial - young[rows, :] * increment).astype(BF16)
    stress = stress_all[...]
    sums_out[...] = dot(high[...], stress) + dot(low[...], stress) - applied[...]


def first_kernel(xi, *rest):
    constitutive(xi[...].reshape(M, -1).astype(BF16), *rest)


def next_kernel(entries, core_ref, mine, other, xi, *rest):
    *rest, xi_out, stress_all, xi_low = rest
    core = core_ref[0]
    factor = factor_of(mine, other, entries)
    for peer in range(mine.shape[0]):
        for source, spot in ((mine, 2 * peer + core), (other, 2 * peer + 1 - core)):
            value = xi[spot] - source[peer, :CHUNK] * factor
            xi_out[spot] = value
            xi_low[spot] = value.astype(BF16)
    constitutive(xi_low[...].reshape(M, -1), *rest, stress_all)


def last_kernel(entries, core_ref, place, mine, other, xi, out):
    factor = factor_of(mine, other, entries)
    chunk = place[0] // 2
    half = pl.ds(pl.multiple_of(place[0] % 2 * 8, 8), 8)
    here = chunk % 2 == core_ref[0]
    delta = jnp.where(here, mine[chunk // 2, half], other[chunk // 2, half])
    out[...] = xi[chunk, half] - delta * factor


def relay_kernel(pieces, out):
    total = pieces[0]
    for peer in range(1, pieces.shape[0]):
        total = total + pieces[peer]
    for peer in range(out.shape[0]):
        out[peer] = total


def close_kernel(load, pieces, out):
    loads = pieces.shape[0] // 2
    squares = jnp.zeros((8, out.shape[2]), F32)
    for group in range(loads):
        total = pieces[group] + pieces[loads + group]
        square = total * total
        squares = squares + square[:8] + square[8:]
    delta = pieces[load[0]] + pieces[loads + load[0]]
    for peer in range(out.shape[0]):
        out[peer, :CHUNK] = delta
        out[peer, CHUNK:] = squares


def shards(
    reduced_shape_matrix,
    young_modulus,
    work_stiffening_modulus,
    entry_flow_stress,
    dilation_factor,
    heat_difference,
    flowing_entry_flags,
    starting_permanent_deformation,
    starting_weights,
    applied_reduced_vector,
    approx_tangent_inverse,
):
    rows, points = starting_permanent_deformation.shape
    own_rows = starting_weights.shape[0]
    size = lax.axis_size
    entries = M * points * size("load")
    place = lax.axis_index(VOX).reshape(1)
    core = lax.axis_index("core").reshape(1)
    load = lax.axis_index("load").reshape(1)
    exchange = functools.partial(lax.all_to_all, split_axis=0, concat_axis=0, tiled=True)

    (weights,) = call(send_kernel, "send", [((size(VOX), own_rows, points), F32)], 3, 1)(
        place, core, load, starting_weights
    )
    xi = exchange(weights, VOX).reshape(CHUNKS, CHUNK, points)

    square = (8, rows // 8)
    wide = ((rows, points), F32)
    fixed = call(
        prepare_kernel,
        "prepare",
        [((M, rows), BF16), ((M, rows), BF16), ((M, points), F32), wide, wide, wide, wide, wide],
        1,
        9,
        [pltpu.VMEM((128, points), F32)],
        1,
    )(
        place,
        approx_tangent_inverse,
        reduced_shape_matrix,
        young_modulus.reshape(square),
        work_stiffening_modulus.reshape(square),
        entry_flow_stress.reshape(square),
        dilation_factor.reshape(square),
        heat_difference.reshape(1, points),
        flowing_entry_flags,
        applied_reduced_vector,
        xi,
    )
    plastic = starting_permanent_deformation
    stress_room = pltpu.VMEM((rows, points), BF16)
    sums_shape = ((M, points), F32)
    xi_shape = ((CHUNKS, CHUNK, points), F32)

    mine = other = None
    for sweep in range(ITERS):
        if sweep == 0:
            plastic, sums = call(first_kernel, "first", [wide, sums_shape], 0, 11, [stress_room])(
                xi, reduced_shape_matrix, *fixed, plastic
            )
        else:
            plastic, sums, xi = call(
                functools.partial(next_kernel, entries),
                "next",
                [wide, sums_shape, xi_shape],
                1,
                13,
                [stress_room, pltpu.VMEM(xi_shape[0], BF16)],
            )(core, mine, other, xi, reduced_shape_matrix, *fixed, plastic)
        pieces = exchange(sums.reshape(CHUNKS, CHUNK, points), COLUMNS)
        (ring,) = call(relay_kernel, "relay", [((size(RING), CHUNK, points), F32)], 0, 1)(pieces)
        ring = exchange(ring, RING)
        (message,) = call(close_kernel, "close", [((size(PLANE), CHUNK + 8, points), F32)], 1, 1)(load, ring)
        mine = exchange(message, PLANE)
        other = lax.ppermute(mine, "core", SWAP)
    (xi_own,) = call(
        functools.partial(last_kernel, entries), "last", [((own_rows, points), F32)], 2, 3
    )(core, place, mine, other, xi)
    return (xi_own, plastic)


def solution(mesh):
    split = Mesh(
        mesh.devices.reshape(4, 2, 4, 2, mesh.shape["load"]),
        ("x", "zl", "y", "core", "load"),
    )
    return jax.shard_map(
        shards,
        mesh=split,
        in_specs=(
            P(VOX, None),
            P(VOX),
            P(VOX),
            P(VOX),
            P(VOX),
            P("load"),
            P(VOX, "load"),
            P(VOX, "load"),
            P(VOX, "load"),
            P(VOX, "load"),
            P(),
        ),
        out_specs=(P(VOX, "load"), P(VOX, "load")),
        check_vma=False,
    )
```

time: 171 us -> 144 us (0.84)
  blocking collectives: 85.2 us -> 120 us
  starting transfers between devices: 30.2 us -> 8.61 us
  matrix products: 16 us -> 0 us
  waiting for transfers between devices: 16.8 us -> 3.21 us
  other arithmetic: 10 us -> 0 us
  Pallas kernels: 0 us -> 6.59 us
  local copies, waits for them, and re-layouts: 8.86 us -> 3.88 us
  between operations: 3.08 us -> 0.79 us
    all_to_all x8 -> x10, blocking collectives: 85.2 us -> 120 us  [the longest x3 38.6 us: shards(): pieces = exchange(sums.reshape(CHUNKS, CHUNK, points), COLUMNS)]
    all_to_all x2 -> x0, starting transfers between devices: 17.6 us -> none  [to_everyone(): lax.all_to_all(jnp.broadcast_to(block[None], (size, *block.shape)), axes,...]
    dot_general x12 -> x0, matrix products: 16 us -> none  [the longest x11 14.3 us: dot(): lax.dot_general(a, b, (dims, ((), ())), preferred_element_type=jnp.float32)]
    all_to_all x2 -> x0, waiting for transfers between devices: 11.1 us -> none  [to_everyone(): lax.all_to_all(jnp.broadcast_to(block[None], (size, *block.shape)), axes,...]
    pallas_call x0 -> x12, Pallas kernels: none -> 6.59 us  [the longest x2 3.1 us: shards(): call(functools.partial(next_kernel, entries), 'next', [wide, sums_shape,...]
    ppermute x6 -> x3, starting transfers between devices: 12.6 us -> 8.61 us  [shards(): other = lax.ppermute(mine, 'core', SWAP)]
    reduce_sum x12 -> x0, other arithmetic: 3.98 us -> none  [the longest x3 2 us: shards(): spread = jnp.sum(pairs[:, :, CHUNK, 0]) / entries]
    ppermute x6 -> x3, waiting for transfers between devices: 5.67 us -> 3.21 us  [shards(): other = lax.ppermute(mine, 'core', SWAP)]
  transfers between devices with their start and end apart: 8 -> 3, of which waited for: 8 -> 3; matrix products, arithmetic and copies ran while one was open for 3% -> 0% of each run, Pallas kernels for 0% -> 0%
where the time goes in v2:
time: 144 us; the launch traced here: 143 us
  blocking collectives  120 us (83%)
  starting transfers between devices  8.61 us (6%)
  Pallas kernels  6.59 us (5%)
  local copies, waits for them, and re-layouts  3.88 us (3%)
  waiting for transfers between devices  3.21 us (2%)
    all_to_all x3, blocking collectives, shards(): pieces = exchange(sums.reshape(CHUNKS, CHUNK, points), COLUMNS)  38.6 us
    all_to_all x3, blocking collectives, shards(): ring = exchange(ring, RING)  32 us
    all_to_all x3, blocking collectives, shards(): mine = exchange(message, PLANE)  29.3 us
    all_to_all x1, blocking collectives, shards(): xi = exchange(weights, VOX).reshape(CHUNKS, CHUNK, points)  20 us
    ppermute x3, starting transfers between devices, shards(): other = lax.ppermute(mine, 'core', SWAP)  8.61 us
    unnamed x24, local copies, waits for them, and re-layouts  3.88 us
    ppermute x3, waiting for transfers between devices, shards(): other = lax.ppermute(mine, 'core', SWAP)  3.21 us
    pallas_call x2, Pallas kernels, shards(): call(functools.partial(next_kernel, entries), 'next', [wide, sums_shape,...  3.1 us
  transfers between devices with their start and end apart: 3, of which 3 were waited for; matrix products, arithmetic and copies ran while one was open for 0% of the time, Pallas kernels for 0%

profile of v2, /device:TPU:1, one launch (start us, length us, event | category | flops | bytes accessed | tf_op | source)
XLA Modules:
  0.0 143.1 jit_solution(7277220369765793862)
XLA Ops:
  0.7 0.7 copy-done.5
  1.5 20.0 %all_to_all.50 = f32[64,8,128]{2,1,0:T(8,128)S(1)} all-to-all(f32[64,8,128]{2,1,0:T(8,128)S(1)} %send.1), channel_id=1, replica_groups=mesh['x'=4,'zl'=2,'y'=4,'core'=2,'load'=4] {'x','zl','y','core'}, dimensions={0} | all-to-all | bytes 524288 | tf_op jit(solution)/shard_map/all_to_all | solution.py:182
  22.2 1.2 copy-done
  23.4 1.2 copy-done.2
  24.7 1.5 %prepare.1 = (bf16[512,1024]{1,0:T(8,128)(2,1)S(1)}, bf16[512,1024]{1,0:T(8,128)(2,1)S(1)}, f32[512,128]{1,0:T(8,128)S(1)}, f32[1024,128]{1,0:T(8,128)S(1)}, f32...) custom-call(s32[1]{0:T(128)} %bitcast.1.place, ...), custom_call_target="tpu_custom_call" | custom-call | tf_op jit(solution)/shard_map/prepare/pallas_call | solution.py:186
  26.2 1.0 first.1
  27.3 12.9 %all_to_all.51.pieces = f32[32,16,128]{2,1,0:T(8,128)S(1)} all-to-all(f32[32,16,128]{2,1,0:T(8,128)S(1)} %bitcast.17), channel_id=1, replica_groups=mesh['x'=4,'zl'=2,'y'=4,'core'=2,'load'=4] {'x','y','core'}, dimensions={0} | all-to-all | bytes 524288 | tf_op jit(solution)/shard_map/all_to_all | solution.py:227
  40.2 13.7 %all_to_all.52.pieces = f32[8,16,128]{2,1,0:T(8,128)S(1)} all-to-all(f32[8,16,128]{2,1,0:T(8,128)S(1)} %relay.3), channel_id=1, replica_groups=mesh['x'=4,'zl'=2,'y'=4,'core'=2,'load'=4] {'zl','load'}, dimensions={0} | all-to-all | bytes 131072 | tf_op jit(solution)/shard_map/all_to_all | solution.py:229
  53.9 9.9 %all_to_all.53.mine = f32[16,24,128]{2,1,0:T(8,128)S(1)} all-to-all(f32[16,24,128]{2,1,0:T(8,128)S(1)} %close.3), channel_id=1, replica_groups=mesh['x'=4,'zl'=2,'y'=4,'core'=2,'load'=4] {'x','y'}, dimensions={0} | all-to-all | bytes 393216 | tf_op jit(solution)/shard_map/all_to_all | solution.py:231
  63.8 3.0 %collective-permute-start = (f32[16,24,128]{2,1,0:T(8,128)S(1)}, f32[16,24,128]{2,1,0:T(8,128)S(1)}, u32[]{:S(2)}, u32[]{:S(2)}) collective-permute-start(f32[16,24,128]{2,1,0:T(8,128)S(1)} %all_to_all.53.mine), channel_id=1, source_target_pairs={{0,4},{4,0},{1,5},{5,1},{2,6},{6,2},{3,7},{7,3},{8,12},{12,8},{9,1... | collective-permute-start | bytes 589832 | tf_op jit(solution)/shard_map/ppermute | solution.py:232
  66.8 1.1 collective-permute-done.other
  67.9 1.2 next.2
  69.1 12.9 %all_to_all.54.pieces = f32[32,16,128]{2,1,0:T(8,128)S(1)} all-to-all(f32[32,16,128]{2,1,0:T(8,128)S(1)} %bitcast.16), channel_id=1, replica_groups=mesh['x'=4,'zl'=2,'y'=4,'core'=2,'load'=4] {'x','y','core'}, dimensions={0} | all-to-all | bytes 524288 | tf_op jit(solution)/shard_map/all_to_all | solution.py:227
  82.1 9.1 %all_to_all.55.pieces = f32[8,16,128]{2,1,0:T(8,128)S(1)} all-to-all(f32[8,16,128]{2,1,0:T(8,128)S(1)} %relay.4), channel_id=1, replica_groups=mesh['x'=4,'zl'=2,'y'=4,'core'=2,'load'=4] {'zl','load'}, dimensions={0} | all-to-all | bytes 131072 | tf_op jit(solution)/shard_map/all_to_all | solution.py:229
  91.2 9.7 %all_to_all.56.mine = f32[16,24,128]{2,1,0:T(8,128)S(1)} all-to-all(f32[16,24,128]{2,1,0:T(8,128)S(1)} %close.4), channel_id=1, replica_groups=mesh['x'=4,'zl'=2,'y'=4,'core'=2,'load'=4] {'x','y'}, dimensions={0} | all-to-all | bytes 393216 | tf_op jit(solution)/shard_map/all_to_all | solution.py:231
  100.9 2.8 %collective-permute-start.1 = (f32[16,24,128]{2,1,0:T(8,128)S(1)}, f32[16,24,128]{2,1,0:T(8,128)S(1)}, u32[]{:S(2)}, u32[]{:S(2)}) collective-permute-start(f32[16,24,128]{2,1,0:T(8,128)S(1)} %all_to_all.56.mine), channel_id=1, source_target_pairs={{0,4},{4,0},{1,5},{5,1},{2,6},{6,2},{3,7},{7,3},{8,12},{12,8},{9,1... | collective-permute-start | bytes 589832 | tf_op jit(solution)/shard_map/ppermute | solution.py:232
  103.7 1.1 collective-permute-done.1.other
  104.8 1.9 %next.3 = (f32[1024,128]{1,0:T(8,128)}, f32[512,128]{1,0:T(8,128)S(1)}, f32[32,16,128]{2,1,0:T(8,128)S(1)}) custom-call(s32[1]{0:T(128)} %bitcast.core.core_ref, f32[16,24,128]{2,1,0:T(8,128)S(1)} %all_to_all.56.mine, f32[16,24,128]{2,1,0:T(8,128)S(1)} %collective-permute-done.1.other, f32[32,16,128]{2,1,0:T(8,128)S(1)} %get-tuple-element.29.xi, ...), custom_call_target="tpu_custom_call" | custom-call | tf_op jit(solution)/shard_map/next/pallas_call | solution.py:219
  106.7 12.9 %all_to_all.57.pieces = f32[32,16,128]{2,1,0:T(8,128)S(1)} all-to-all(f32[32,16,128]{2,1,0:T(8,128)S(1)} %bitcast.15), channel_id=1, replica_groups=mesh['x'=4,'zl'=2,'y'=4,'core'=2,'load'=4] {'x','y','core'}, dimensions={0} | all-to-all | bytes 524288 | tf_op jit(solution)/shard_map/all_to_all | solution.py:227
  119.6 9.1 %all_to_all.58.pieces = f32[8,16,128]{2,1,0:T(8,128)S(1)} all-to-all(f32[8,16,128]{2,1,0:T(8,128)S(1)} %relay.5), channel_id=1, replica_groups=mesh['x'=4,'zl'=2,'y'=4,'core'=2,'load'=4] {'zl','load'}, dimensions={0} | all-to-all | bytes 131072 | tf_op jit(solution)/shard_map/all_to_all | solution.py:229
  128.8 9.7 %all_to_all.59.mine = f32[16,24,128]{2,1,0:T(8,128)S(1)} all-to-all(f32[16,24,128]{2,1,0:T(8,128)S(1)} %close.5), channel_id=1, replica_groups=mesh['x'=4,'zl'=2,'y'=4,'core'=2,'load'=4] {'x','y'}, dimensions={0} | all-to-all | bytes 393216 | tf_op jit(solution)/shard_map/all_to_all | solution.py:231
  138.5 2.8 %collective-permute-start.2 = (f32[16,24,128]{2,1,0:T(8,128)S(1)}, f32[16,24,128]{2,1,0:T(8,128)S(1)}, u32[]{:S(2)}, u32[]{:S(2)}) collective-permute-start(f32[16,24,128]{2,1,0:T(8,128)S(1)} %all_to_all.59.mine), channel_id=1, source_target_pairs={{0,4},{4,0},{1,5},{5,1},{2,6},{6,2},{3,7},{7,3},{8,12},{12,8},{9,1... | collective-permute-start | bytes 589832 | tf_op jit(solution)/shard_map/ppermute | solution.py:232
  141.3 1.1 collective-permute-done.2.other
  142.3 0.8 last.1
  (28 shorter events, 0.9 us)
Async XLA Ops:
  0.6 20.9 %copy-start.3 = (s32[1024,128]{1,0:T(8,128)S(1)}, s32[1024,128]{1,0:T(8,128)}, u32[]{:S(2)}) copy-start(s32[1024,128]{1,0:T(8,128)} %flags.1) | copy-start | bytes 1572868
  0.7 0.7 copy-start.5
  1.4 20.1 %copy-start.8 = (f32[1024]{0:T(1024)S(1)}, f32[1024]{0:T(1024)}, u32[]{:S(2)}) copy-start(f32[1024]{0:T(1024)} %param.14) | copy-start | bytes 12292
  1.4 20.1 %copy-start.9 = (f32[1024]{0:T(1024)S(1)}, f32[1024]{0:T(1024)}, u32[]{:S(2)}) copy-start(f32[1024]{0:T(1024)} %param.15) | copy-start | bytes 12292
  1.4 20.1 %copy-start.10 = (f32[8,128]{1,0:T(8,128)S(1)}, f32[8,128]{1,0:T(8,128)}, u32[]{:S(2)}) copy-start(f32[8,128]{1,0:T(8,128)} %applied.1) | copy-start | bytes 12292
  21.5 0.7 copy-start.7
  21.5 0.7 copy-start.6
  21.5 0.7 copy-start.11
  22.2 1.2 copy-start
  23.4 1.2 copy-start.2
  24.7 1.5 %copy-start.1 = (bf16[1024,512]{1,0:T(8,128)(2,1)S(1)}, bf16[1024,512]{1,0:T(8,128)(2,1)}, u32[]{:S(2)}) copy-start(bf16[1024,512]{1,0:T(8,128)(2,1)} %rest_0_.5) | copy-start | bytes 3145732
  24.7 1.6 %copy-start.4 = (f32[1024,128]{1,0:T(8,128)S(1)}, f32[1024,128]{1,0:T(8,128)}, u32[]{:S(2)}) copy-start(f32[1024,128]{1,0:T(8,128)} %rest_9_.1) | copy-start | bytes 1572868
  63.8 4.1 %collective-permute-start = (f32[16,24,128]{2,1,0:T(8,128)S(1)}, f32[16,24,128]{2,1,0:T(8,128)S(1)}, u32[]{:S(2)}, u32[]{:S(2)}) collective-permute-start(f32[16,24,128]{2,1,0:T(8,128)S(1)} %all_to_all.53.mine), channel_id=1, source_target_pairs={{0,4},{4,0},{1,5},{5,1},{2,6},{6,2},{3,7},{7,3},{8,12},{12,8},{9,1... | collective-permute-start | bytes 589832 | tf_op jit(solution)/shard_map/ppermute | solution.py:232
  100.9 3.9 %collective-permute-start.1 = (f32[16,24,128]{2,1,0:T(8,128)S(1)}, f32[16,24,128]{2,1,0:T(8,128)S(1)}, u32[]{:S(2)}, u32[]{:S(2)}) collective-permute-start(f32[16,24,128]{2,1,0:T(8,128)S(1)} %all_to_all.56.mine), channel_id=1, source_target_pairs={{0,4},{4,0},{1,5},{5,1},{2,6},{6,2},{3,7},{7,3},{8,12},{12,8},{9,1... | collective-permute-start | bytes 589832 | tf_op jit(solution)/shard_map/ppermute | solution.py:232
  138.5 3.9 %collective-permute-start.2 = (f32[16,24,128]{2,1,0:T(8,128)S(1)}, f32[16,24,128]{2,1,0:T(8,128)S(1)}, u32[]{:S(2)}, u32[]{:S(2)}) collective-permute-start(f32[16,24,128]{2,1,0:T(8,128)S(1)} %all_to_all.59.mine), channel_id=1, source_target_pairs={{0,4},{4,0},{1,5},{5,1},{2,6},{6,2},{3,7},{7,3},{8,12},{12,8},{9,1... | collective-permute-start | bytes 589832 | tf_op jit(solution)/shard_map/ppermute | solution.py:232

commit v3 on v2

--- a/solution.py
+++ b/solution.py
@@ -20,18 +20,17 @@
 BLOCK = 128
 
 HERE = pl.BlockSpec(memory_space=pltpu.VMEM)
-ANYWHERE = pl.BlockSpec(memory_space=pl.ANY)
 SCALAR = pl.BlockSpec(memory_space=pltpu.SMEM)
 F32 = jnp.float32
 BF16 = jnp.bfloat16
 
 
-def call(kernel, name, outs, n_scalars, n_arrays, scratch=(), n_unread=0):
+def call(kernel, name, outs, n_scalars, n_arrays, scratch=()):
     return pl.pallas_call(
         kernel,
         name=name,
         out_shape=[jax.ShapeDtypeStruct(*out) for out in outs],
-        in_specs=[SCALAR] * n_scalars + [HERE] * n_arrays + [ANYWHERE] * n_unread,
+        in_specs=[SCALAR] * n_scalars + [HERE] * n_arrays,
         out_specs=[HERE] * len(outs),
         scratch_shapes=list(scratch),
         compiler_params=pltpu.CompilerParams(vmem_limit_bytes=16 << 20),
@@ -53,8 +52,8 @@
 
 
 def prepare_kernel(
-    place, inverse, basis, young, harden, flow, dilate, heat, flags, applied, after,
-    high_out, low_out, applied_out, young_out, flow_out, inv_flow_out, weight_out, heat_out,
+    place, inverse, basis, young, harden, flow, dilate, heat, flags, applied, plastic,
+    map_out, applied_out, columns_out, heat_out, active_out,
     padded,
 ):
     inverse_high, inverse_low = split_two(inverse[...])
@@ -62,29 +61,24 @@
         rows = slice(block, block + 256)
         part = basis[rows, :]
         both = dot(inverse_high, part, ((1,), (1,))) + dot(inverse_low, part, ((1,), (1,)))
-        high, low = split_two(both)
-        high_out[:, rows] = high
-        low_out[:, rows] = low
+        map_out[:, rows] = both.astype(BF16)
+    heat_out[...] = heat[...]
+    active_out[...] = flags[...].astype(BF16)
     padded[...] = jnp.zeros_like(padded)
     padded[pl.ds(pl.multiple_of(place[0] % 16 * 8, 8), 8), :] = applied[...]
     columns = inverse[:, pl.ds(pl.multiple_of(place[0] // 16 * 128, 128), 128)]
     a_high, a_low = split_two(columns)
     b_high, b_low = split_two(padded[...])
     applied_out[...] = dot(a_high, b_high) + (dot(a_high, b_low) + dot(a_low, b_high))
-    young_t = young[...].T
-    flow_t = flow[...].T
-    inv_flow_t = (1.0 / flow[...]).T
-    weight_t = (1.0 / (young[...] + harden[...])).T
-    dilate_t = dilate[...].T
-    for block in range(8):
-        rows = slice(block * 128, block * 128 + 128)
-        column = slice(block, block + 1)
-        wide = (128, 128)
-        young_out[rows, :] = jnp.broadcast_to(young_t[:, column], wide)
-        flow_out[rows, :] = jnp.broadcast_to(flow_t[:, column], wide)
-        inv_flow_out[rows, :] = jnp.broadcast_to(inv_flow_t[:, column], wide)
-        weight_out[rows, :] = flags[rows, :].astype(F32) * weight_t[:, column]
-        heat_out[rows, :] = dilate_t[:, column] * heat[...]
+    factors = (
+        young[...] / flow[...],
+        flow[...],
+        young[...],
+        flow[...] / (young[...] + harden[...]),
+        dilate[...],
+    )
+    spare = jnp.zeros((128 - 8 * len(factors), 128), F32)
+    columns_out[...] = jnp.concatenate([*factors, spare], axis=0).T
 
 
 def factor_of(mine, other, entries):
@@ -95,17 +89,18 @@
     return 1.0 / (1.0 + spread)
 
 
-def constitutive(xi_now, basis, high, low, applied, young, flow, inv_flow, weight, heat, plastic, plastic_out, sums_out, stress_all):
-    for block in range(0, basis.shape[0], BLOCK):
-        rows = slice(block, block + BLOCK)
+def constitutive(xi_now, basis, map_in, applied, columns, heat, active, plastic, plastic_out, sums_out, stress_all):
+    for block in range(basis.shape[0] // BLOCK):
+        rows = slice(block * BLOCK, block * BLOCK + BLOCK)
+        slope, flow, young, weight, dilate = (
+            columns[:, 8 * factor + block : 8 * factor + block + 1] for factor in range(5)
+        )
         strain = dot(basis[rows, :], xi_now)
-        trial = young[rows, :] * (strain - heat[rows, :] - plastic[rows, :])
-        excess = trial - flow[rows, :] * jnp.tanh(trial * inv_flow[rows, :])
-        increment = weight[rows, :] * excess
+        ratio = slope * (strain - dilate * heat[...] - plastic[rows, :])
+        increment = active[rows, :].astype(F32) * weight * (ratio - jnp.tanh(ratio))
         plastic_out[rows, :] = plastic[rows, :] + increment
-        stress_all[rows, :] = (trial - young[rows, :] * increment).astype(BF16)
-    stress = stress_all[...]
-    sums_out[...] = dot(high[...], stress) + dot(low[...], stress) - applied[...]
+        stress_all[rows, :] = (flow * ratio - young * increment).astype(BF16)
+    sums_out[...] = dot(map_in[...], stress_all[...]) - applied[...]
 
 
 def first_kernel(xi, *rest):
@@ -186,11 +181,10 @@
     fixed = call(
         prepare_kernel,
         "prepare",
-        [((M, rows), BF16), ((M, rows), BF16), ((M, points), F32), wide, wide, wide, wide, wide],
+        [((M, rows), BF16), ((M, points), F32), ((128, 128), F32), ((1, points), F32), ((rows, points), BF16)],
         1,
-        9,
+        10,
         [pltpu.VMEM((128, points), F32)],
-        1,
     )(
         place,
         approx_tangent_inverse,
@@ -202,7 +196,7 @@
         heat_difference.reshape(1, points),
         flowing_entry_flags,
         applied_reduced_vector,
-        xi,
+        starting_permanent_deformation,
     )
     plastic = starting_permanent_deformation
     stress_room = pltpu.VMEM((rows, points), BF16)
@@ -212,7 +206,7 @@
     mine = other = None
     for sweep in range(ITERS):
         if sweep == 0:
-            plastic, sums = call(first_kernel, "first", [wide, sums_shape], 0, 11, [stress_room])(
+            plastic, sums = call(first_kernel, "first", [wide, sums_shape], 0, 8, [stress_room])(
                 xi, reduced_shape_matrix, *fixed, plastic
             )
         else:
@@ -221,7 +215,7 @@
                 "next",
                 [wide, sums_shape, xi_shape],
                 1,
-                13,
+                10,
                 [stress_room, pltpu.VMEM(xi_shape[0], BF16)],
             )(core, mine, other, xi, reduced_shape_matrix, *fixed, plastic)
         pieces = exchange(sums.reshape(CHUNKS, CHUNK, points), COLUMNS)

time: 144 us -> 140 us (0.972)
  blocking collectives: 120 us -> 100 us
  starting transfers between devices: 8.61 us -> 19.1 us
  waiting for transfers between devices: 3.21 us -> 7.37 us
    all_to_all x1 -> x0, blocking collectives: 20 us -> none  [shards(): xi = exchange(weights, VOX).reshape(CHUNKS, CHUNK, points)]
    all_to_all x0 -> x1, starting transfers between devices: none -> 10.5 us  [shards(): xi = exchange(weights, VOX).reshape(CHUNKS, CHUNK, points)]
    all_to_all x0 -> x1, waiting for transfers between devices: none -> 4.16 us  [shards(): xi = exchange(weights, VOX).reshape(CHUNKS, CHUNK, points)]
  transfers between devices with their start and end apart: 3 -> 4, of which waited for: 3 -> 4; matrix products, arithmetic and copies ran while one was open for 0% -> 0% of each run, Pallas kernels for 0% -> 1%
where the time goes in v3:
time: 140 us
  blocking collectives  100 us (71%)
  starting transfers between devices  19.1 us (14%)
  Pallas kernels  7.48 us (5%)
  waiting for transfers between devices  7.37 us (5%)
  local copies, waits for them, and re-layouts  4.89 us (3%)
    all_to_all x3, blocking collectives, shards(): pieces = exchange(sums.reshape(CHUNKS, CHUNK, points), COLUMNS)  38.6 us
    all_to_all x3, blocking collectives, shards(): ring = exchange(ring, RING)  32 us
    all_to_all x3, blocking collectives, shards(): mine = exchange(message, PLANE)  29.3 us
    all_to_all x1, starting transfers between devices, shards(): xi = exchange(weights, VOX).reshape(CHUNKS, CHUNK, points)  10.5 us
    ppermute x3, starting transfers between devices, shards(): other = lax.ppermute(mine, 'core', SWAP)  8.61 us
    unnamed x24, local copies, waits for them, and re-layouts  4.89 us
    all_to_all x1, waiting for transfers between devices, shards(): xi = exchange(weights, VOX).reshape(CHUNKS, CHUNK, points)  4.16 us
    ppermute x3, waiting for transfers between devices, shards(): other = lax.ppermute(mine, 'core', SWAP)  3.21 us
  transfers between devices with their start and end apart: 4, of which 4 were waited for; matrix products, arithmetic and copies ran while one was open for 0% of the time, Pallas kernels for 1%

profile of v3, /device:TPU:1, one launch (start us, length us, event | category | flops | bytes accessed | tf_op | source)
XLA Modules:
  0.0 139.6 jit_solution(11572589488527093789)
XLA Ops:
  2.1 10.5 %all-to-all-start = ((f32[64,8,128]{2,1,0:T(8,128)}), f32[64,8,128]{2,1,0:T(8,128)S(1)}, u32[]{:S(2)}, u32[]{:S(2)}) async-start(f32[64,8,128]{2,1,0:T(8,128)} %send.1), calls=%async_computation | async-start | bytes 524288 | tf_op jit(solution)/shard_map/all_to_all | solution.py:177
  13.3 1.2 copy-done
  14.5 1.2 copy-done.3
  15.8 1.0 copy-done.4
  16.8 1.4 %prepare.1 = (bf16[512,1024]{1,0:T(8,128)(2,1)S(1)}, f32[512,128]{1,0:T(8,128)S(1)}, f32[128,128]{1,0:T(8,128)S(1)}, f32[1,128]{1,0:T(1,128)S(1)}, bf16[1024,128]{1,0:T(8,128)(2,1)S(1)}) custom-call(s32[1]{0:T(128)} %bitcast.1.place, f32[512,512]{1,0:T(8,128)S(1)} %copy-done.3, bf16[1024,512]{1,0:T(8,128)(2,1)S(1)} %copy-done, f32[8,128]{1,0:T(8,128)S(1)} %bitcast.17, ...), custom_call_target="tpu_custom_call" | custom-call | tf_op jit(solution)/shard_map/prepare/pallas_call | solution.py:181
  18.2 4.2 %all-to-all-done = f32[64,8,128]{2,1,0:T(8,128)S(1)} async-done(((f32[64,8,128]{2,1,0:T(8,128)}), f32[64,8,128]{2,1,0:T(8,128)S(1)}, u32[]{:S(2)}, u32[]{:S(2)}) %all-to-all-start) | async-done | bytes 262176 | tf_op jit(solution)/shard_map/all_to_all | solution.py:177
  22.4 1.3 first.1
  23.7 12.9 %all_to_all.50.pieces = f32[32,16,128]{2,1,0:T(8,128)S(1)} all-to-all(f32[32,16,128]{2,1,0:T(8,128)S(1)} %bitcast.16), channel_id=1, replica_groups=mesh['x'=4,'zl'=2,'y'=4,'core'=2,'load'=4] {'x','y','core'}, dimensions={0} | all-to-all | bytes 524288 | tf_op jit(solution)/shard_map/all_to_all | solution.py:221
  36.6 13.7 %all_to_all.51.pieces = f32[8,16,128]{2,1,0:T(8,128)S(1)} all-to-all(f32[8,16,128]{2,1,0:T(8,128)S(1)} %relay.3), channel_id=1, replica_groups=mesh['x'=4,'zl'=2,'y'=4,'core'=2,'load'=4] {'zl','load'}, dimensions={0} | all-to-all | bytes 131072 | tf_op jit(solution)/shard_map/all_to_all | solution.py:223
  50.3 9.9 %all_to_all.52.mine = f32[16,24,128]{2,1,0:T(8,128)S(1)} all-to-all(f32[16,24,128]{2,1,0:T(8,128)S(1)} %close.3), channel_id=1, replica_groups=mesh['x'=4,'zl'=2,'y'=4,'core'=2,'load'=4] {'x','y'}, dimensions={0} | all-to-all | bytes 393216 | tf_op jit(solution)/shard_map/all_to_all | solution.py:225
  60.2 3.0 %collective-permute-start = (f32[16,24,128]{2,1,0:T(8,128)S(1)}, f32[16,24,128]{2,1,0:T(8,128)S(1)}, u32[]{:S(2)}, u32[]{:S(2)}) collective-permute-start(f32[16,24,128]{2,1,0:T(8,128)S(1)} %all_to_all.52.mine), channel_id=1, source_target_pairs={{0,4},{4,0},{1,5},{5,1},{2,6},{6,2},{3,7},{7,3},{8,12},{12,8},{9,1... | collective-permute-start | bytes 589832 | tf_op jit(solution)/shard_map/ppermute | solution.py:226
  63.2 1.1 collective-permute-done.other
  64.3 1.3 next.2
  65.6 12.9 %all_to_all.53.pieces = f32[32,16,128]{2,1,0:T(8,128)S(1)} all-to-all(f32[32,16,128]{2,1,0:T(8,128)S(1)} %bitcast.15), channel_id=1, replica_groups=mesh['x'=4,'zl'=2,'y'=4,'core'=2,'load'=4] {'x','y','core'}, dimensions={0} | all-to-all | bytes 524288 | tf_op jit(solution)/shard_map/all_to_all | solution.py:221
  78.6 9.1 %all_to_all.54.pieces = f32[8,16,128]{2,1,0:T(8,128)S(1)} all-to-all(f32[8,16,128]{2,1,0:T(8,128)S(1)} %relay.4), channel_id=1, replica_groups=mesh['x'=4,'zl'=2,'y'=4,'core'=2,'load'=4] {'zl','load'}, dimensions={0} | all-to-all | bytes 131072 | tf_op jit(solution)/shard_map/all_to_all | solution.py:223
  87.7 9.7 %all_to_all.55.mine = f32[16,24,128]{2,1,0:T(8,128)S(1)} all-to-all(f32[16,24,128]{2,1,0:T(8,128)S(1)} %close.4), channel_id=1, replica_groups=mesh['x'=4,'zl'=2,'y'=4,'core'=2,'load'=4] {'x','y'}, dimensions={0} | all-to-all | bytes 393216 | tf_op jit(solution)/shard_map/all_to_all | solution.py:225
  97.4 2.8 %collective-permute-start.1 = (f32[16,24,128]{2,1,0:T(8,128)S(1)}, f32[16,24,128]{2,1,0:T(8,128)S(1)}, u32[]{:S(2)}, u32[]{:S(2)}) collective-permute-start(f32[16,24,128]{2,1,0:T(8,128)S(1)} %all_to_all.55.mine), channel_id=1, source_target_pairs={{0,4},{4,0},{1,5},{5,1},{2,6},{6,2},{3,7},{7,3},{8,12},{12,8},{9,1... | collective-permute-start | bytes 589832 | tf_op jit(solution)/shard_map/ppermute | solution.py:226
  100.2 1.1 collective-permute-done.1.other
  101.3 1.8 %next.3 = (f32[1024,128]{1,0:T(8,128)}, f32[512,128]{1,0:T(8,128)S(1)}, f32[32,16,128]{2,1,0:T(8,128)S(1)}) custom-call(s32[1]{0:T(128)} %bitcast.core.core_ref, f32[16,24,128]{2,1,0:T(8,128)S(1)} %all_to_all.55.mine, f32[16,24,128]{2,1,0:T(8,128)S(1)} %collective-permute-done.1.other, f32[32,16,128]{2,1,0:T(8,128)S(1)} %get-tuple-element.23.xi, ...), custom_call_target="tpu_custom_call" | custom-call | tf_op jit(solution)/shard_map/next/pallas_call | solution.py:213
  103.2 12.9 %all_to_all.56.pieces = f32[32,16,128]{2,1,0:T(8,128)S(1)} all-to-all(f32[32,16,128]{2,1,0:T(8,128)S(1)} %bitcast.14), channel_id=1, replica_groups=mesh['x'=4,'zl'=2,'y'=4,'core'=2,'load'=4] {'x','y','core'}, dimensions={0} | all-to-all | bytes 524288 | tf_op jit(solution)/shard_map/all_to_all | solution.py:221
  116.1 9.1 %all_to_all.57.pieces = f32[8,16,128]{2,1,0:T(8,128)S(1)} all-to-all(f32[8,16,128]{2,1,0:T(8,128)S(1)} %relay.5), channel_id=1, replica_groups=mesh['x'=4,'zl'=2,'y'=4,'core'=2,'load'=4] {'zl','load'}, dimensions={0} | all-to-all | bytes 131072 | tf_op jit(solution)/shard_map/all_to_all | solution.py:223
  125.2 9.7 %all_to_all.58.mine = f32[16,24,128]{2,1,0:T(8,128)S(1)} all-to-all(f32[16,24,128]{2,1,0:T(8,128)S(1)} %close.5), channel_id=1, replica_groups=mesh['x'=4,'zl'=2,'y'=4,'core'=2,'load'=4] {'x','y'}, dimensions={0} | all-to-all | bytes 393216 | tf_op jit(solution)/shard_map/all_to_all | solution.py:225
  134.9 2.8 %collective-permute-start.2 = (f32[16,24,128]{2,1,0:T(8,128)S(1)}, f32[16,24,128]{2,1,0:T(8,128)S(1)}, u32[]{:S(2)}, u32[]{:S(2)}) collective-permute-start(f32[16,24,128]{2,1,0:T(8,128)S(1)} %all_to_all.58.mine), channel_id=1, source_target_pairs={{0,4},{4,0},{1,5},{5,1},{2,6},{6,2},{3,7},{7,3},{8,12},{12,8},{9,1... | collective-permute-start | bytes 589832 | tf_op jit(solution)/shard_map/ppermute | solution.py:226
  137.7 1.1 collective-permute-done.2.other
  (29 shorter events, 3.0 us)
Async XLA Ops:
  0.6 12.0 %copy-start.2 = (f32[1024,128]{1,0:T(8,128)S(1)}, f32[1024,128]{1,0:T(8,128)}, u32[]{:S(2)}) copy-start(f32[1024,128]{1,0:T(8,128)} %rest_6_.1) | copy-start | bytes 1572868
  0.7 0.7 copy-start.5
  2.1 10.5 %copy-start.8 = (f32[1024]{0:T(1024)S(1)}, f32[1024]{0:T(1024)}, u32[]{:S(2)}) copy-start(f32[1024]{0:T(1024)} %param.14) | copy-start | bytes 12292
  2.1 10.5 %copy-start.9 = (f32[1024]{0:T(1024)S(1)}, f32[1024]{0:T(1024)}, u32[]{:S(2)}) copy-start(f32[1024]{0:T(1024)} %param.15) | copy-start | bytes 12292
  2.1 10.5 %copy-start.10 = (f32[8,128]{1,0:T(8,128)S(1)}, f32[8,128]{1,0:T(8,128)}, u32[]{:S(2)}) copy-start(f32[8,128]{1,0:T(8,128)} %applied.1) | copy-start | bytes 12292
  2.1 20.3 %all-to-all-start = ((f32[64,8,128]{2,1,0:T(8,128)}), f32[64,8,128]{2,1,0:T(8,128)S(1)}, u32[]{:S(2)}, u32[]{:S(2)}) async-start(f32[64,8,128]{2,1,0:T(8,128)} %send.1), calls=%async_computation | async-start | bytes 524288 | tf_op jit(solution)/shard_map/all_to_all | solution.py:177
  12.6 0.7 copy-start.7
  12.6 0.7 copy-start.6
  12.6 0.7 copy-start.11
  13.3 1.2 copy-start
  14.5 1.2 copy-start.3
  15.8 1.0 copy-start.4
  16.8 5.6 %copy-start.1 = (bf16[1024,512]{1,0:T(8,128)(2,1)S(1)}, bf16[1024,512]{1,0:T(8,128)(2,1)}, u32[]{:S(2)}) copy-start(bf16[1024,512]{1,0:T(8,128)(2,1)} %rest_0_.5) | copy-start | bytes 3145732
  60.2 4.1 %collective-permute-start = (f32[16,24,128]{2,1,0:T(8,128)S(1)}, f32[16,24,128]{2,1,0:T(8,128)S(1)}, u32[]{:S(2)}, u32[]{:S(2)}) collective-permute-start(f32[16,24,128]{2,1,0:T(8,128)S(1)} %all_to_all.52.mine), channel_id=1, source_target_pairs={{0,4},{4,0},{1,5},{5,1},{2,6},{6,2},{3,7},{7,3},{8,12},{12,8},{9,1... | collective-permute-start | bytes 589832 | tf_op jit(solution)/shard_map/ppermute | solution.py:226
  97.4 3.9 %collective-permute-start.1 = (f32[16,24,128]{2,1,0:T(8,128)S(1)}, f32[16,24,128]{2,1,0:T(8,128)S(1)}, u32[]{:S(2)}, u32[]{:S(2)}) collective-permute-start(f32[16,24,128]{2,1,0:T(8,128)S(1)} %all_to_all.55.mine), channel_id=1, source_target_pairs={{0,4},{4,0},{1,5},{5,1},{2,6},{6,2},{3,7},{7,3},{8,12},{12,8},{9,1... | collective-permute-start | bytes 589832 | tf_op jit(solution)/shard_map/ppermute | solution.py:226
  134.9 3.9 %collective-permute-start.2 = (f32[16,24,128]{2,1,0:T(8,128)S(1)}, f32[16,24,128]{2,1,0:T(8,128)S(1)}, u32[]{:S(2)}, u32[]{:S(2)}) collective-permute-start(f32[16,24,128]{2,1,0:T(8,128)S(1)} %all_to_all.58.mine), channel_id=1, source_target_pairs={{0,4},{4,0},{1,5},{5,1},{2,6},{6,2},{3,7},{7,3},{8,12},{12,8},{9,1... | collective-permute-start | bytes 589832 | tf_op jit(solution)/shard_map/ppermute | solution.py:226

commit v4 on v3

--- a/solution.py
+++ b/solution.py
@@ -11,8 +11,8 @@
 M = 512
 ITERS = 3
 VOX = ("x", "zl", "y", "core")
-PLANE = ("x", "y")
-COLUMNS = ("x", "y", "core")
+PLANE = ("y", "x")
+COLUMNS = ("core", "y", "x")
 RING = ("zl", "load")
 SWAP = [(0, 1), (1, 0)]
 CHUNK = 16
@@ -25,11 +25,11 @@
 BF16 = jnp.bfloat16
 
 
-def call(kernel, name, outs, n_scalars, n_arrays, scratch=()):
+def call(kernel, name, outs, n_scalars, n_arrays, scratch=(), stay=False):
     return pl.pallas_call(
         kernel,
         name=name,
-        out_shape=[jax.ShapeDtypeStruct(*out) for out in outs],
+        out_shape=[(pltpu.VMEM if stay else jax.ShapeDtypeStruct)(*out) for out in outs],
         in_specs=[SCALAR] * n_scalars + [HERE] * n_arrays,
         out_specs=[HERE] * len(outs),
         scratch_shapes=list(scratch),
@@ -111,8 +111,9 @@
     *rest, xi_out, stress_all, xi_low = rest
     core = core_ref[0]
     factor = factor_of(mine, other, entries)
-    for peer in range(mine.shape[0]):
-        for source, spot in ((mine, 2 * peer + core), (other, 2 * peer + 1 - core)):
+    peers = mine.shape[0]
+    for peer in range(peers):
+        for source, spot in ((mine, peers * core + peer), (other, peers * (1 - core) + peer)):
             value = xi[spot] - source[peer, :CHUNK] * factor
             xi_out[spot] = value
             xi_low[spot] = value.astype(BF16)
@@ -123,8 +124,9 @@
     factor = factor_of(mine, other, entries)
     chunk = place[0] // 2
     half = pl.ds(pl.multiple_of(place[0] % 2 * 8, 8), 8)
-    here = chunk % 2 == core_ref[0]
-    delta = jnp.where(here, mine[chunk // 2, half], other[chunk // 2, half])
+    peer = chunk % mine.shape[0]
+    here = chunk // mine.shape[0] == core_ref[0]
+    delta = jnp.where(here, mine[peer, half], other[peer, half])
     out[...] = xi[chunk, half] - delta * factor
 
 
@@ -217,6 +219,7 @@
                 1,
                 10,
                 [stress_room, pltpu.VMEM(xi_shape[0], BF16)],
+                True,
             )(core, mine, other, xi, reduced_shape_matrix, *fixed, plastic)
         pieces = exchange(sums.reshape(CHUNKS, CHUNK, points), COLUMNS)
         (ring,) = call(relay_kernel, "relay", [((size(RING), CHUNK, points), F32)], 0, 1)(pieces)

time: 140 us -> 139 us (level)
    all_to_all x3, blocking collectives: 38.6 us -> 35.8 us  [shards(): pieces = exchange(sums.reshape(CHUNKS, CHUNK, points), COLUMNS)]
    all_to_all x3, blocking collectives: 29.3 us -> 32 us  [shards(): mine = exchange(message, PLANE)]
    unnamed x24 -> x25, local copies, waits for them, and re-layouts: 4.89 us -> 5.68 us
  transfers between devices with their start and end apart: 4 -> 4, of which waited for: 4 -> 4; matrix products, arithmetic and copies ran while one was open for 0% -> 1% of each run, Pallas kernels for 1% -> 1%
where the time goes in v4:
time: 139 us
  blocking collectives  99.8 us (72%)
  starting transfers between devices  18.8 us (14%)
  Pallas kernels  6.97 us (5%)
  waiting for transfers between devices  6.58 us (5%)
  local copies, waits for them, and re-layouts  5.68 us (4%)
    all_to_all x3, blocking collectives, shards(): pieces = exchange(sums.reshape(CHUNKS, CHUNK, points), COLUMNS)  35.8 us
    all_to_all x3, blocking collectives, shards(): ring = exchange(ring, RING)  32.1 us
    all_to_all x3, blocking collectives, shards(): mine = exchange(message, PLANE)  32 us
    all_to_all x1, starting transfers between devices, shards(): xi = exchange(weights, VOX).reshape(CHUNKS, CHUNK, points)  10.5 us
    ppermute x3, starting transfers between devices, shards(): other = lax.ppermute(mine, 'core', SWAP)  8.36 us
    unnamed x25, local copies, waits for them, and re-layouts  5.68 us
    all_to_all x1, waiting for transfers between devices, shards(): xi = exchange(weights, VOX).reshape(CHUNKS, CHUNK, points)  4.16 us
  transfers between devices with their start and end apart: 4, of which 4 were waited for; matrix products, arithmetic and copies ran while one was open for 1% of the time, Pallas kernels for 1%

profile of v4, /device:TPU:1, one launch (start us, length us, event | category | flops | bytes accessed | tf_op | source)
XLA Modules:
  0.0 138.7 jit_solution(9947447142082774203)
XLA Ops:
  2.1 10.5 %all-to-all-start = ((f32[64,8,128]{2,1,0:T(8,128)}), f32[64,8,128]{2,1,0:T(8,128)S(1)}, u32[]{:S(2)}, u32[]{:S(2)}) async-start(f32[64,8,128]{2,1,0:T(8,128)} %send.1), calls=%async_computation | async-start | bytes 524288 | tf_op jit(solution)/shard_map/all_to_all | solution.py:179
  13.3 1.2 copy-done
  14.5 1.2 copy-done.3
  15.8 1.0 copy-done.4
  16.8 1.4 %prepare.1 = (bf16[512,1024]{1,0:T(8,128)(2,1)S(1)}, f32[512,128]{1,0:T(8,128)S(1)}, f32[128,128]{1,0:T(8,128)S(1)}, f32[1,128]{1,0:T(1,128)S(1)}, bf16[1024,128]{1,0:T(8,128)(2,1)S(1)}) custom-call(s32[1]{0:T(128)} %bitcast.1.place, f32[512,512]{1,0:T(8,128)S(1)} %copy-done.3, bf16[1024,512]{1,0:T(8,128)(2,1)S(1)} %copy-done, f32[8,128]{1,0:T(8,128)S(1)} %bitcast.17, ...), custom_call_target="tpu_custom_call" | custom-call | tf_op jit(solution)/shard_map/prepare/pallas_call | solution.py:183
  18.2 4.2 %all-to-all-done = f32[64,8,128]{2,1,0:T(8,128)S(1)} async-done(((f32[64,8,128]{2,1,0:T(8,128)}), f32[64,8,128]{2,1,0:T(8,128)S(1)}, u32[]{:S(2)}, u32[]{:S(2)}) %all-to-all-start) | async-done | bytes 262176 | tf_op jit(solution)/shard_map/all_to_all | solution.py:179
  22.4 1.3 first.1
  23.7 12.3 %all_to_all.50.pieces = f32[32,16,128]{2,1,0:T(8,128)S(1)} all-to-all(f32[32,16,128]{2,1,0:T(8,128)S(1)} %bitcast.16), channel_id=1, replica_groups=mesh['x'=4,'zl'=2,'y'=4,'core'=2,'load'=4] {'core','y','x'}, dimensions={0} | all-to-all | bytes 524288 | tf_op jit(solution)/shard_map/all_to_all | solution.py:224
  35.9 13.8 %all_to_all.51.pieces = f32[8,16,128]{2,1,0:T(8,128)S(1)} all-to-all(f32[8,16,128]{2,1,0:T(8,128)S(1)} %relay.3), channel_id=1, replica_groups=mesh['x'=4,'zl'=2,'y'=4,'core'=2,'load'=4] {'zl','load'}, dimensions={0} | all-to-all | bytes 131072 | tf_op jit(solution)/shard_map/all_to_all | solution.py:226
  49.8 10.5 %all_to_all.52.mine = f32[16,24,128]{2,1,0:T(8,128)S(1)} all-to-all(f32[16,24,128]{2,1,0:T(8,128)S(1)} %close.3), channel_id=1, replica_groups=mesh['x'=4,'zl'=2,'y'=4,'core'=2,'load'=4] {'y','x'}, dimensions={0} | all-to-all | bytes 393216 | tf_op jit(solution)/shard_map/all_to_all | solution.py:228
  60.3 3.2 %collective-permute-start = (f32[16,24,128]{2,1,0:T(8,128)S(1)}, f32[16,24,128]{2,1,0:T(8,128)S(1)}, u32[]{:S(2)}, u32[]{:S(2)}) collective-permute-start(f32[16,24,128]{2,1,0:T(8,128)S(1)} %all_to_all.52.mine), channel_id=1, source_target_pairs={{0,4},{4,0},{1,5},{5,1},{2,6},{6,2},{3,7},{7,3},{8,12},{12,8},{9,1... | collective-permute-start | bytes 589832 | tf_op jit(solution)/shard_map/ppermute | solution.py:229
  63.4 1.1 collective-permute-done.other
  64.5 1.3 next.2
  65.9 11.8 %all_to_all.53.pieces = f32[32,16,128]{2,1,0:T(8,128)S(1)} all-to-all(f32[32,16,128]{2,1,0:T(8,128)S(1)} %bitcast.15), channel_id=1, replica_groups=mesh['x'=4,'zl'=2,'y'=4,'core'=2,'load'=4] {'core','y','x'}, dimensions={0} | all-to-all | bytes 524288 | tf_op jit(solution)/shard_map/all_to_all | solution.py:224
  77.7 9.1 %all_to_all.54.pieces = f32[8,16,128]{2,1,0:T(8,128)S(1)} all-to-all(f32[8,16,128]{2,1,0:T(8,128)S(1)} %relay.4), channel_id=1, replica_groups=mesh['x'=4,'zl'=2,'y'=4,'core'=2,'load'=4] {'zl','load'}, dimensions={0} | all-to-all | bytes 131072 | tf_op jit(solution)/shard_map/all_to_all | solution.py:226
  86.8 10.7 %all_to_all.55.mine = f32[16,24,128]{2,1,0:T(8,128)S(1)} all-to-all(f32[16,24,128]{2,1,0:T(8,128)S(1)} %close.4), channel_id=1, replica_groups=mesh['x'=4,'zl'=2,'y'=4,'core'=2,'load'=4] {'y','x'}, dimensions={0} | all-to-all | bytes 393216 | tf_op jit(solution)/shard_map/all_to_all | solution.py:228
  97.6 2.6 %collective-permute-start.1 = (f32[16,24,128]{2,1,0:T(8,128)S(1)}, f32[16,24,128]{2,1,0:T(8,128)S(1)}, u32[]{:S(2)}, u32[]{:S(2)}) collective-permute-start(f32[16,24,128]{2,1,0:T(8,128)S(1)} %all_to_all.55.mine), channel_id=1, source_target_pairs={{0,4},{4,0},{1,5},{5,1},{2,6},{6,2},{3,7},{7,3},{8,12},{12,8},{9,1... | collective-permute-start | bytes 589832 | tf_op jit(solution)/shard_map/ppermute | solution.py:229
  100.1 1.1 collective-permute-done.1.other
  101.2 1.3 next.3
  102.5 11.8 %all_to_all.56.pieces = f32[32,16,128]{2,1,0:T(8,128)S(1)} all-to-all(f32[32,16,128]{2,1,0:T(8,128)S(1)} %bitcast.14), channel_id=1, replica_groups=mesh['x'=4,'zl'=2,'y'=4,'core'=2,'load'=4] {'core','y','x'}, dimensions={0} | all-to-all | bytes 524288 | tf_op jit(solution)/shard_map/all_to_all | solution.py:224
  114.3 9.1 %all_to_all.57.pieces = f32[8,16,128]{2,1,0:T(8,128)S(1)} all-to-all(f32[8,16,128]{2,1,0:T(8,128)S(1)} %relay.5), channel_id=1, replica_groups=mesh['x'=4,'zl'=2,'y'=4,'core'=2,'load'=4] {'zl','load'}, dimensions={0} | all-to-all | bytes 131072 | tf_op jit(solution)/shard_map/all_to_all | solution.py:226
  123.5 10.7 %all_to_all.58.mine = f32[16,24,128]{2,1,0:T(8,128)S(1)} all-to-all(f32[16,24,128]{2,1,0:T(8,128)S(1)} %close.5), channel_id=1, replica_groups=mesh['x'=4,'zl'=2,'y'=4,'core'=2,'load'=4] {'y','x'}, dimensions={0} | all-to-all | bytes 393216 | tf_op jit(solution)/shard_map/all_to_all | solution.py:228
  134.2 2.6 %collective-permute-start.2 = (f32[16,24,128]{2,1,0:T(8,128)S(1)}, f32[16,24,128]{2,1,0:T(8,128)S(1)}, u32[]{:S(2)}, u32[]{:S(2)}) collective-permute-start(f32[16,24,128]{2,1,0:T(8,128)S(1)} %all_to_all.58.mine), channel_id=1, source_target_pairs={{0,4},{4,0},{1,5},{5,1},{2,6},{6,2},{3,7},{7,3},{8,12},{12,8},{9,1... | collective-permute-start | bytes 589832 | tf_op jit(solution)/shard_map/ppermute | solution.py:229
  136.8 0.8 copy.13
  (30 shorter events, 3.3 us)
Async XLA Ops:
  0.6 12.0 %copy-start.2 = (f32[1024,128]{1,0:T(8,128)S(1)}, f32[1024,128]{1,0:T(8,128)}, u32[]{:S(2)}) copy-start(f32[1024,128]{1,0:T(8,128)} %rest_6_.1) | copy-start | bytes 1572868
  0.7 0.7 copy-start.5
  2.1 10.5 %copy-start.8 = (f32[1024]{0:T(1024)S(1)}, f32[1024]{0:T(1024)}, u32[]{:S(2)}) copy-start(f32[1024]{0:T(1024)} %param.14) | copy-start | bytes 12292
  2.1 10.5 %copy-start.9 = (f32[1024]{0:T(1024)S(1)}, f32[1024]{0:T(1024)}, u32[]{:S(2)}) copy-start(f32[1024]{0:T(1024)} %param.15) | copy-start | bytes 12292
  2.1 10.5 %copy-start.10 = (f32[8,128]{1,0:T(8,128)S(1)}, f32[8,128]{1,0:T(8,128)}, u32[]{:S(2)}) copy-start(f32[8,128]{1,0:T(8,128)} %applied.1) | copy-start | bytes 12292
  2.1 20.3 %all-to-all-start = ((f32[64,8,128]{2,1,0:T(8,128)}), f32[64,8,128]{2,1,0:T(8,128)S(1)}, u32[]{:S(2)}, u32[]{:S(2)}) async-start(f32[64,8,128]{2,1,0:T(8,128)} %send.1), calls=%async_computation | async-start | bytes 524288 | tf_op jit(solution)/shard_map/all_to_all | solution.py:179
  12.6 0.7 copy-start.7
  12.6 0.7 copy-start.6
  12.6 0.7 copy-start.11
  13.3 1.2 copy-start
  14.5 1.2 copy-start.3
  15.8 1.0 copy-start.4
  16.8 5.6 %copy-start.1 = (bf16[1024,512]{1,0:T(8,128)(2,1)S(1)}, bf16[1024,512]{1,0:T(8,128)(2,1)}, u32[]{:S(2)}) copy-start(bf16[1024,512]{1,0:T(8,128)(2,1)} %rest_0_.5) | copy-start | bytes 3145732
  60.3 4.3 %collective-permute-start = (f32[16,24,128]{2,1,0:T(8,128)S(1)}, f32[16,24,128]{2,1,0:T(8,128)S(1)}, u32[]{:S(2)}, u32[]{:S(2)}) collective-permute-start(f32[16,24,128]{2,1,0:T(8,128)S(1)} %all_to_all.52.mine), channel_id=1, source_target_pairs={{0,4},{4,0},{1,5},{5,1},{2,6},{6,2},{3,7},{7,3},{8,12},{12,8},{9,1... | collective-permute-start | bytes 589832 | tf_op jit(solution)/shard_map/ppermute | solution.py:229
  97.6 3.7 %collective-permute-start.1 = (f32[16,24,128]{2,1,0:T(8,128)S(1)}, f32[16,24,128]{2,1,0:T(8,128)S(1)}, u32[]{:S(2)}, u32[]{:S(2)}) collective-permute-start(f32[16,24,128]{2,1,0:T(8,128)S(1)} %all_to_all.55.mine), channel_id=1, source_target_pairs={{0,4},{4,0},{1,5},{5,1},{2,6},{6,2},{3,7},{7,3},{8,12},{12,8},{9,1... | collective-permute-start | bytes 589832 | tf_op jit(solution)/shard_map/ppermute | solution.py:229
  134.2 3.7 %collective-permute-start.2 = (f32[16,24,128]{2,1,0:T(8,128)S(1)}, f32[16,24,128]{2,1,0:T(8,128)S(1)}, u32[]{:S(2)}, u32[]{:S(2)}) collective-permute-start(f32[16,24,128]{2,1,0:T(8,128)S(1)} %all_to_all.58.mine), channel_id=1, source_target_pairs={{0,4},{4,0},{1,5},{5,1},{2,6},{6,2},{3,7},{7,3},{8,12},{12,8},{9,1... | collective-permute-start | bytes 589832 | tf_op jit(solution)/shard_map/ppermute | solution.py:229
